TPU v7x, 32 devices: a whole 2x2x4 slice. The times are simulated.
32 devices in a mesh: seq: 8 (over z, y), tensor: 4 (over x, core).
Axes of the slice: x: 2, y: 2, z: 4, core: 2. Of those that a mesh axis runs over, the one named last changes fastest.
Arguments:
- queries: bfloat16 [2048, 8192], P('seq', 'tensor'), may hold values from -4 to 4, as said below
- keys: bfloat16 [2048, 1024], P('seq', 'tensor'), may hold values from -96 to 96, as said below
- values: bfloat16 [2048, 1024], P('seq', 'tensor'), may hold values from -6 to 6
- block_pos: int32 [16], replicated, may hold values from 0 to 15, each once
Outputs:
- attended: bfloat16 [2048, 8192], P('seq')
Inputs may be any that keep to these rules, and one draw needn't show every extreme that they name: block_pos is a permutation of 0 to 15. real-valued queries. real-valued keys.
All inputs are finite; a program needn't handle non-finite values.
Results may differ from a plain program's by a relative error of at most 0.004.
Values may be sent and summed in bfloat16 or wider, within the bound.
No kernel may reach another device: no remote copies, remote signals or barrier semaphores. Data moves between devices by JAX's collectives and lax.ppermute only.
A program may use at most 64 MiB of HBM per device.

v0:
```python
import math

import jax
import jax.numpy as jnp
from jax import lax
from jax.sharding import PartitionSpec as P

QUERY_HEADS = 64
KEY_VALUE_HEADS = 8
HEAD_WIDTH = 128
VISIBLE_SHARDS = 4


def from_behind(block, axis, distance):
    devices = range(lax.axis_size(axis))
    route = [((i - distance) % len(devices), i) for i in devices]
    return lax.ppermute(block, axis, route)


def shard_positions(block_pos, shard, block_len):
    pair = lax.dynamic_slice_in_dim(block_pos, 2 * shard, 2, 0)
    offsets = jnp.arange(block_len, dtype=jnp.int32)
    return (pair[:, None] * block_len + offsets[None, :]).reshape(-1)


def attend(query_rows, q_pos, key_gathered, value_gathered, key_pos):
    rows = query_rows.shape[0]
    groups = key_gathered.shape[1]
    group_factor = QUERY_HEADS // KEY_VALUE_HEADS
    q_heads = query_rows.reshape(rows, groups, group_factor, HEAD_WIDTH)
    scores = jnp.einsum("qgrd,kgd->grqk", q_heads, key_gathered, preferred_element_type=jnp.float32)
    scores = scores * (1.0 / math.sqrt(HEAD_WIDTH))
    allowed = key_pos[None, :] <= q_pos[:, None]
    scores = jnp.where(allowed[None, None], scores, -1e30)
    top = jnp.max(scores, axis=-1, keepdims=True)
    weights = jnp.exp(scores - top)
    total = jnp.sum(weights, axis=-1)
    rounded = weights.astype(jnp.bfloat16)
    mixed = jnp.einsum(
        "grqk,kgd->qgrd", rounded, value_gathered, preferred_element_type=jnp.float32
    )
    mixed = mixed / jnp.transpose(total, (2, 0, 1))[..., None]
    return mixed.reshape(rows, groups * group_factor * HEAD_WIDTH).astype(jnp.bfloat16)


def body(queries, keys, values, block_pos):
    tok_rows = queries.shape[0]
    block_len = tok_rows // 2
    groups = keys.shape[1] // HEAD_WIDTH
    shard = lax.axis_index("seq")
    count = lax.axis_size("seq")
    stacked = jnp.stack([keys, values])
    pieces = [stacked]
    current = stacked
    for back in range(1, VISIBLE_SHARDS):
        current = from_behind(current, "seq", 1)
        pieces.append(current)
    key_gathered = jnp.concatenate([piece[0] for piece in pieces], 0).reshape(
        VISIBLE_SHARDS * tok_rows, groups, HEAD_WIDTH
    )
    value_gathered = jnp.concatenate([piece[1] for piece in pieces], 0).reshape(
        VISIBLE_SHARDS * tok_rows, groups, HEAD_WIDTH
    )
    key_pos = jnp.concatenate(
        [
            shard_positions(block_pos, (shard - back) % count, block_len)
            for back in range(VISIBLE_SHARDS)
        ],
        0,
    )
    q_pos = shard_positions(block_pos, shard, block_len)
    halves = []
    for half in range(2):
        q_part = queries[half * block_len : (half + 1) * block_len]
        pos_part = q_pos[half * block_len : (half + 1) * block_len]
        local = attend(q_part, pos_part, key_gathered, value_gathered, key_pos)
        halves.append(lax.all_gather(local, "tensor", axis=1, tiled=True))
    return jnp.concatenate(halves, 0)


def solution(mesh):
    placed = (P("seq", "tensor"), P("seq", "tensor"), P("seq", "tensor"), P())
    return jax.shard_map(
        body, mesh=mesh, in_specs=placed, out_specs=P("seq", None), check_vma=False
    )
```

profile of v0, /device:TPU:0, one launch (start us, length us, event | category | flops | bytes accessed | tf_op | source)
XLA Modules:
  0.0 102.2 jit_solution(1030988277564516786)
XLA Ops:
  6.5 0.0 all-gather.5.cloned.1.call-start
  6.5 1.0 copy.14
  7.5 1.0 copy.13
  8.6 3.0 %collective-permute-start = (bf16[2,256,256]{1,2,0:T(8,128)(2,1)S(1)}, bf16[2,256,256]{1,2,0:T(8,128)(2,1)S(1)}, u32[]{:S(2)}, u32[]{:S(2)}) collective-permute-start(bf16[2,256,256]{1,2,0:T(8,128)(2,1)S(1)} %pad_maximum_fusion.1), channel_id=1, source_target_pairs={{28,0},{0,4},{4,8},{8,12},{12,16},{16,20},{20,24},{24,28},{29,1},{... | collective-permute-start | bytes 786440 | tf_op jit(solution)/shard_map/ppermute | solution.py:17
  11.6 0.9 dynamic-slice_multiply_fusion.4
  12.6 0.1 iota_add_fusion
  12.6 1.3 %fusion.32 = (bf16[128,2048]{1,0:T(8,128)(2,1)S(1)}, bf16[128,2048]{1,0:T(8,128)(2,1)S(1)}) fusion(bf16[256,2048]{1,0:T(8,128)(2,1)} %param.4), kind=kLoop, calls=%fused_computation.47 | loop fusion | bytes 2097152 | tf_op jit(solution)/shard_map/slice | solution.py:74
  13.9 0.1 add_bitcast_fusion.2
  14.0 0.1 add_bitcast_fusion
  14.0 6.9 %collective-permute-done = bf16[2,256,256]{1,2,0:T(8,128)(2,1)S(1)} collective-permute-done((bf16[2,256,256]{1,2,0:T(8,128)(2,1)S(1)}, bf16[2,256,256]{1,2,0:T(8,128)(2,1)S(1)}, u32[]{:S(2)}, u32[]{:S(2)}) %collective-permute-start) | collective-permute-done | bytes 262176 | tf_op jit(solution)/shard_map/ppermute | solution.py:17
  21.0 0.0 collective-permute-start.1
  21.0 0.1 copy.17
  21.1 0.3 copy.36
  21.4 0.2 broadcast_compare_fusion.1
  21.6 9.5 %collective-permute-done.1 = bf16[2,256,256]{1,2,0:T(8,128)(2,1)S(1)} collective-permute-done((bf16[2,256,256]{1,2,0:T(8,128)(2,1)S(1)}, bf16[2,256,256]{1,2,0:T(8,128)(2,1)S(1)}, u32[]{:S(2)}, u32[]{:S(2)}) %collective-permute-start.1) | collective-permute-done | bytes 262176 | tf_op jit(solution)/shard_map/ppermute | solution.py:17
  31.2 0.0 collective-permute-start.2
  31.2 0.1 copy.18
  31.3 0.1 copy.19
  31.5 9.0 %collective-permute-done.2 = bf16[2,256,256]{1,2,0:T(8,128)(2,1)S(1)} collective-permute-done((bf16[2,256,256]{1,2,0:T(8,128)(2,1)S(1)}, bf16[2,256,256]{1,2,0:T(8,128)(2,1)S(1)}, u32[]{:S(2)}, u32[]{:S(2)}) %collective-permute-start.2) | collective-permute-done | bytes 262176 | tf_op jit(solution)/shard_map/ppermute | solution.py:17
  40.5 0.1 copy.20
  40.6 1.3 %fusion.5 = (f32[2,8,128]{2,1,0:T(8,128)S(1)}, f32[2,1024,128,8]{2,1,3,0:T(8,128)S(1)}) fusion(pred[128,1024]{0,1:T(8,128)(4,1)S(1)} %get-tuple-element.14, bf16[128,2,8,128]{0,3,2,1:T(8,128)(2,1)S(1)} %bitcast.82, bf16[256,2,128]{2,0,1:T(8,128)(2,1)S(1)} %copy.20, bf16[256,2,128]{2,0,1:T(8,128)(2,1)S(1)} %copy.19, bf16[256,2,128]{2,0,1:T(8,128)(2,1)S(1)} %copy.18, ...), kind=kOutput, calls=%fused_computation.9 | convolution fusion | flops 545257472 | bytes 9576448 | tf_op jit(solution)/shard_map/qgrd,kgd->grqk/dot_general | solution.py:31
  41.9 1.7 %fusion.2 = f32[2,8,128]{2,1,0:T(8,128)S(1)} fusion(f32[2,1024,128,8]{2,1,3,0:T(8,128)S(1)} %get-tuple-element.23, f32[2,8,128]{2,1,0:T(8,128)S(1)} %get-tuple-element.22, pred[128,1024]{0,1:T(8,128)(4,1)S(1)} %get-tuple-element.14), kind=kLoop, calls=%fused_computation.6 | loop fusion | flops 8386560 | bytes 8536064 | tf_op jit(solution)/shard_map/reduce_sum | solution.py:37
  43.7 2.2 %divide_convert_fusion = bf16[128,2,8,128]{0,3,2,1:T(8,128)(2,1)S(1)} fusion(f32[2,1024,128,8]{2,1,3,0:T(8,128)S(1)} %get-tuple-element.23, f32[2,8,128]{2,1,0:T(8,128)S(1)} %get-tuple-element.22, pred[128,1024]{0,1:T(8,128)(4,1)S(1)} %get-tuple-element.14, f32[128,2,8]{0,2,1:T(8,128)S(1)} %bitcast.99, bf16[256,2,128]{0,2,1:T(8,128)(2,1)S(1)} %bitcast.96, ...), kind=kOutput, calls=%fused_computation.17 | convolution fusion | flops 547880960 | bytes 9584640 | tf_op jit(solution)/shard_map/grqk,kgd->qgrd/dot_general | solution.py:39
  45.8 1.0 copy.28
  46.8 0.0 all-gather.5.cloned.1.call-update
  46.9 0.2 all-gather.3.cloned.1.call-start
  47.1 0.3 copy.35
  47.4 1.3 %fusion.4 = (f32[2,8,128]{2,1,0:T(8,128)S(1)}, f32[2,1024,128,8]{2,1,3,0:T(8,128)S(1)}) fusion(pred[128,1024]{0,1:T(8,128)(4,1)S(1)} %get-tuple-element.13, bf16[128,2,8,128]{0,3,2,1:T(8,128)(2,1)S(1)} %bitcast.83, bf16[256,2,128]{2,0,1:T(8,128)(2,1)S(1)} %copy.20, bf16[256,2,128]{2,0,1:T(8,128)(2,1)S(1)} %copy.19, bf16[256,2,128]{2,0,1:T(8,128)(2,1)S(1)} %copy.18, ...), kind=kOutput, calls=%fused_computation.8 | convolution fusion | flops 545257472 | bytes 9576448 | tf_op jit(solution)/shard_map/qgrd,kgd->grqk/dot_general | solution.py:31
  48.7 1.7 %fusion = f32[2,8,128]{2,1,0:T(8,128)S(1)} fusion(f32[2,1024,128,8]{2,1,3,0:T(8,128)S(1)} %get-tuple-element.25, f32[2,8,128]{2,1,0:T(8,128)S(1)} %get-tuple-element.24, pred[128,1024]{0,1:T(8,128)(4,1)S(1)} %get-tuple-element.13), kind=kLoop, calls=%fused_computation.4 | loop fusion | flops 8386560 | bytes 8536064 | tf_op jit(solution)/shard_map/reduce_sum | solution.py:37
  50.4 2.2 %divide_convert_fusion.1 = bf16[128,2,8,128]{0,3,2,1:T(8,128)(2,1)S(1)} fusion(f32[2,1024,128,8]{2,1,3,0:T(8,128)S(1)} %get-tuple-element.25, f32[2,8,128]{2,1,0:T(8,128)S(1)} %get-tuple-element.24, pred[128,1024]{0,1:T(8,128)(4,1)S(1)} %get-tuple-element.13, f32[128,2,8]{0,2,1:T(8,128)S(1)} %bitcast.98, bf16[256,2,128]{0,2,1:T(8,128)(2,1)S(1)} %bitcast.97, ...), kind=kOutput, calls=%fused_computation.18 | convolution fusion | flops 547880960 | bytes 9584640 | tf_op jit(solution)/shard_map/grqk,kgd->qgrd/dot_general | solution.py:39
  52.6 1.0 %copy.24 = bf16[128,2048]{1,0:T(8,128)(2,1)} copy(bf16[128,2048]{0,1:T(8,128)(2,1)S(1)} %bitcast.84) | data formatting | bytes 1048576 | tf_op jit(solution)/shard_map/convert_element_type | solution.py:43
  53.6 0.0 all-gather.3.cloned.1.call-update
  53.7 12.9 %all-gather.5.cloned.1.call-done = bf16[128,8192]{1,0:T(8,128)(2,1)} async-done(((bf16[128,2048]{1,0:T(8,128)(2,1)}), bf16[128,8192]{1,0:T(8,128)(2,1)}) %all-gather.5.cloned.1.call-update) | async-done | bytes 2097168 | tf_op jit(solution)/shard_map/all_gather | solution.py:77
  66.5 24.2 %all-gather.3.cloned.1.call-done = bf16[128,8192]{1,0:T(8,128)(2,1)} async-done(((bf16[128,2048]{1,0:T(8,128)(2,1)}), bf16[128,8192]{1,0:T(8,128)(2,1)}) %all-gather.3.cloned.1.call-update) | async-done | bytes 2097168 | tf_op jit(solution)/shard_map/all_gather | solution.py:77
  90.7 4.7 %pad_maximum_fusion = bf16[256,8192]{1,0:T(8,128)(2,1)} fusion(bf16[128,8192]{1,0:T(8,128)(2,1)} %all-gather.5.cloned.1.call-done, bf16[128,8192]{1,0:T(8,128)(2,1)} %all-gather.3.cloned.1.call-done), kind=kLoop, calls=%fused_computation.10 | loop fusion | flops 8388608 | bytes 8388608 | tf_op jit(solution)/shard_map/concatenate | solution.py:78
  (6 shorter events, 0.1 us)
Async XLA Ops:
  6.5 60.0 %all-gather.5.cloned.1.call-start = ((), (), s32[]{:S(2)}) async-start(), calls=%async_computation.1 | async-start | bytes 2621440 | tf_op jit(solution)/shard_map/all_gather | solution.py:77
  8.6 12.4 %collective-permute-start = (bf16[2,256,256]{1,2,0:T(8,128)(2,1)S(1)}, bf16[2,256,256]{1,2,0:T(8,128)(2,1)S(1)}, u32[]{:S(2)}, u32[]{:S(2)}) collective-permute-start(bf16[2,256,256]{1,2,0:T(8,128)(2,1)S(1)} %pad_maximum_fusion.1), channel_id=1, source_target_pairs={{28,0},{0,4},{4,8},{8,12},{12,16},{16,20},{20,24},{24,28},{29,1},{... | collective-permute-start | bytes 786440 | tf_op jit(solution)/shard_map/ppermute | solution.py:17
  21.0 10.2 %collective-permute-start.1 = (bf16[2,256,256]{1,2,0:T(8,128)(2,1)S(1)}, bf16[2,256,256]{1,2,0:T(8,128)(2,1)S(1)}, u32[]{:S(2)}, u32[]{:S(2)}) collective-permute-start(bf16[2,256,256]{1,2,0:T(8,128)(2,1)S(1)} %collective-permute-done), channel_id=1, source_target_pairs={{28,0},{0,4},{4,8},{8,12},{12,16},{16,20},{20,24},{24,28},{29,1},{... | collective-permute-start | bytes 786440 | tf_op jit(solution)/shard_map/ppermute | solution.py:17
  31.2 9.3 %collective-permute-start.2 = (bf16[2,256,256]{1,2,0:T(8,128)(2,1)S(1)}, bf16[2,256,256]{1,2,0:T(8,128)(2,1)S(1)}, u32[]{:S(2)}, u32[]{:S(2)}) collective-permute-start(bf16[2,256,256]{1,2,0:T(8,128)(2,1)S(1)} %collective-permute-done.1), channel_id=1, source_target_pairs={{28,0},{0,4},{4,8},{8,12},{12,16},{16,20},{20,24},{24,28},{29,1},{... | collective-permute-start | bytes 786440 | tf_op jit(solution)/shard_map/ppermute | solution.py:17
  46.9 43.8 %all-gather.3.cloned.1.call-start = ((), (), s32[]{:S(2)}) async-start(), calls=%async_computation | async-start | bytes 2621440 | tf_op jit(solution)/shard_map/all_gather | solution.py:77
Sparse Core Ops, SparseCore 0:
  47.0 19.4 all-gather.4
  68.1 22.5 all-gather.2
where the time goes:
time: 102 us
  waiting for transfers between devices  62.5 us (61%)
  between operations  13.5 us (13%)
  other arithmetic  9.54 us (9%)
  matrix products  6.94 us (7%)
  local copies, waits for them, and re-layouts  6.4 us (6%)
  starting transfers between devices  3.28 us (3%)
    all_gather x2, waiting for transfers between devices, body(): halves.append(lax.all_gather(local, 'tensor', axis=1, tiled=True))  37 us
    ppermute x3, waiting for transfers between devices, from_behind(): return lax.ppermute(block, axis, route)  25.5 us
    concatenate x1, other arithmetic, body(): return jnp.concatenate(halves, 0)  4.67 us
    dot_general x2, matrix products, attend(): jnp.einsum('grqk,kgd->qgrd', rounded, value_gathered, preferred_element_t...  4.34 us
    reduce_sum x2, other arithmetic, attend(): total = jnp.sum(weights, axis=-1)  3.49 us
    ppermute x3, starting transfers between devices, from_behind(): return lax.ppermute(block, axis, route)  3.05 us
    dot_general x2, matrix products, attend(): jnp.einsum('qgrd,kgd->grqk', q_heads, key_gathered, preferred_element_typ...  2.6 us
    unnamed x4, local copies, waits for them, and re-layouts  2.55 us
  transfers between devices with their start and end apart: 5, of which 5 were waited for; matrix products, arithmetic and copies ran while one was open for 10% of the time, Pallas kernels for 0%

commit v1 on v0

v1 whole, which is shorter than its diff:
```python
import functools
import math

import jax
import jax.numpy as jnp
from jax import lax
from jax.experimental import pallas as pl
from jax.experimental.pallas import tpu as pltpu
from jax.sharding import PartitionSpec as P


QUERY_HEADS = 64
KEY_VALUE_HEADS = 8
HEAD_WIDTH = 128
GROUP = QUERY_HEADS // KEY_VALUE_HEADS
VISIBLE_SHARDS = 4
TILE_HEADS = 2

ANY = pl.BlockSpec(memory_space=pl.ANY)
SMEM = pl.BlockSpec(memory_space=pltpu.SMEM)
LOCAL = pl.BlockSpec(memory_space=pltpu.VMEM)


def shift(x, axis, distance):
    n = lax.axis_size(axis)
    return lax.ppermute(x, axis, [(i, (i + distance) % n) for i in range(n)])


def partner(x, axis):
    n = lax.axis_size(axis)
    return lax.ppermute(x, axis, [(i, i ^ 1) for i in range(n)])


def resident(x):
    return pltpu.with_memory_space_constraint(x, pltpu.VMEM)


def prepare_kernel(pos_ref, q_ref, stack_ref, mask_ref, sems, *, chunks, block_len, count):
    copies = []
    for c in range(chunks):
        g, qb = c // 2, c % 2
        for h in range(GROUP):
            col = (g * GROUP + h) * HEAD_WIDTH
            copies.append(pltpu.make_async_copy(
                q_ref.at[qb * block_len:(qb + 1) * block_len, col:col + HEAD_WIDTH],
                stack_ref.at[c, h * block_len:(h + 1) * block_len, :HEAD_WIDTH],
                sems.at[c * GROUP + h]))
    for copy in copies:
        copy.start()
    ahead = (lax.broadcasted_iota(jnp.int32, (block_len, block_len), 1)
             - lax.broadcasted_iota(jnp.int32, (block_len, block_len), 0))
    unit = jnp.where(ahead == 0, 1.0, 0.0).astype(jnp.bfloat16)
    for c in range(chunks):
        for h in range(GROUP):
            stack_ref[c, h * block_len:(h + 1) * block_len, HEAD_WIDTH:] = unit
    shard = lax.axis_index("seq").astype(jnp.int32)
    for qb in range(2):
        q_block = pos_ref[2 * shard + qb]
        for back in range(VISIBLE_SHARDS):
            source = lax.rem(shard - back + count, count)
            for kb in range(2):
                gap = (pos_ref[2 * source + kb] - q_block) * block_len
                at = (2 * back + kb) * block_len
                mask_ref[qb * block_len:(qb + 1) * block_len, at:at + block_len] = jnp.where(
                    ahead + gap <= 0, 0.0, -1e30).astype(jnp.bfloat16)
    for copy in copies:
        copy.wait()


def prepare(block_pos, queries, groups):
    tok = queries.shape[0]
    block_len = tok // 2
    chunks = 2 * groups
    return pl.pallas_call(
        functools.partial(prepare_kernel, chunks=chunks, block_len=block_len,
                          count=lax.axis_size("seq")),
        in_specs=[SMEM, ANY],
        out_specs=[LOCAL, LOCAL],
        out_shape=[
            pltpu.VMEM((chunks, GROUP * block_len, HEAD_WIDTH + block_len), jnp.bfloat16),
            pltpu.VMEM((tok, VISIBLE_SHARDS * tok), jnp.bfloat16),
        ],
        scratch_shapes=[pltpu.SemaphoreType.DMA((chunks * GROUP,))],
        name="prepare",
    )(block_pos, queries)


def attend_kernel(stack_ref, mask_ref, *rest, chunk, block_len):
    pieces = rest[:VISIBLE_SHARDS]
    out_ref, k_scr, v_scr = rest[VISIBLE_SHARDS:]
    tok = 2 * block_len
    qb = chunk % 2
    for slot, ref in enumerate(pieces):
        k_scr[:HEAD_WIDTH, slot * tok:(slot + 1) * tok] = ref[0].T
        v_scr[slot * tok:(slot + 1) * tok, :HEAD_WIDTH] = ref[1]
    v_scr[:, HEAD_WIDTH:] = jnp.ones((VISIBLE_SHARDS * tok, HEAD_WIDTH), jnp.bfloat16)
    k_scr[HEAD_WIDTH:, :] = mask_ref[qb * block_len:(qb + 1) * block_len, :]
    scale = math.log2(math.e) / math.sqrt(HEAD_WIDTH)
    tile = TILE_HEADS * block_len
    steps = GROUP // TILE_HEADS

    def scores(t):
        q = stack_ref[chunk, t * tile:(t + 1) * tile, :]
        return jnp.dot(q, k_scr[...], preferred_element_type=jnp.float32)

    def finish(t, s):
        top = jnp.max(s, axis=1, keepdims=True)
        w = jnp.exp2((s - top) * scale).astype(jnp.bfloat16)
        o = jnp.dot(w, v_scr[...], preferred_element_type=jnp.float32)
        o = (o[:, :HEAD_WIDTH] / o[:, HEAD_WIDTH:]).astype(jnp.bfloat16)
        for i in range(TILE_HEADS):
            h = t * TILE_HEADS + i
            out_ref[:, h * HEAD_WIDTH:(h + 1) * HEAD_WIDTH] = (
                o[i * block_len:(i + 1) * block_len])

    s = scores(0)
    for t in range(steps):
        following = scores(t + 1) if t + 1 < steps else None
        finish(t, s)
        s = following


def attend(stack, mask, chunk, pieces):
    block_len = mask.shape[0] // 2
    seen = mask.shape[1]
    return pl.pallas_call(
        functools.partial(attend_kernel, chunk=chunk, block_len=block_len),
        in_specs=[LOCAL] * (2 + VISIBLE_SHARDS),
        out_specs=LOCAL,
        out_shape=pltpu.VMEM((block_len, GROUP * HEAD_WIDTH), jnp.bfloat16),
        scratch_shapes=[
            pltpu.VMEM((HEAD_WIDTH + block_len, seen), jnp.bfloat16),
            pltpu.VMEM((seen, 2 * HEAD_WIDTH), jnp.bfloat16),
        ],
    )(resident(stack), resident(mask), *[resident(p) for p in pieces])


def place_kernel(*refs, spots, groups, tensor):
    n = len(spots)
    out, sems = refs[-2:]
    me = lax.axis_index("tensor").astype(jnp.int32)
    copies = []
    for i, (ref, (row, hop, flip, group)) in enumerate(zip(refs[:n], spots)):
        h, w = ref.shape
        owner = lax.rem(me - 2 * hop + tensor, tensor)
        if flip:
            owner = owner + 1 - 2 * lax.rem(owner, 2)
        col = pl.multiple_of((owner * groups + group) * w, w)
        copies.append(pltpu.make_async_copy(
            ref, out.at[pl.ds(row, h), pl.ds(col, w)], sems.at[i]))
    for copy in copies:
        copy.start()
    for copy in copies:
        copy.wait()


def place(out, shape, groups, entries):
    n = len(entries)
    aliased = [] if out is None else [out]
    return pl.pallas_call(
        functools.partial(place_kernel, spots=tuple(e[1:] for e in entries), groups=groups,
                          tensor=lax.axis_size("tensor")),
        in_specs=[LOCAL] * n + [ANY] * len(aliased),
        out_specs=ANY,
        out_shape=jax.ShapeDtypeStruct(shape, jnp.bfloat16),
        input_output_aliases={n: 0} if aliased else {},
        scratch_shapes=[pltpu.SemaphoreType.DMA((n,))],
        name="place",
    )(*[resident(e[0]) for e in entries], *aliased)


def body(queries, keys, values, block_pos):
    tok = queries.shape[0]
    block_len = tok // 2
    groups = keys.shape[1] // HEAD_WIDTH
    tensor = lax.axis_size("tensor")
    shape = (tok, queries.shape[1] * tensor)

    pieces = []
    for g in range(groups):
        at = slice(g * HEAD_WIDTH, (g + 1) * HEAD_WIDTH)
        own = jnp.stack([keys[:, at], values[:, at]])
        behind = [own]
        for back in range(1, VISIBLE_SHARDS):
            behind.append(shift(own, "seq", back))
        pieces.append(behind)
    stack, mask = prepare(block_pos, queries, groups)

    arrivals = []
    beside = []
    for chunk in range(2 * groups):
        g, qb = chunk // 2, chunk % 2
        row = qb * block_len
        local = attend(stack, mask, chunk, pieces[g])
        now = []
        for hop in range(1, tensor // 2):
            now.append((shift(local, "tensor", 2 * hop), row, hop, False, g))
        arrivals.append(now)
        beside.append((local, row, 0, False, g))
        beside.append((partner(local, "tensor"), row, 0, True, g))
    out = place(None, shape, groups, beside)
    for now in arrivals:
        if now:
            first, out = lax.optimization_barrier((now[0][0], out))
            now[0] = (first,) + now[0][1:]
            crossed = [(partner(e[0], "tensor"),) + e[1:3] + (True,) + e[4:] for e in now]
            out = place(out, shape, groups, now + crossed)
    return out


def solution(mesh):
    placed = (P("seq", "tensor"), P("seq", "tensor"), P("seq", "tensor"), P())

    return jax.shard_map(
        body, mesh=mesh, in_specs=placed, out_specs=P("seq", None), check_vma=False
    )
```

time: 102 us -> 79.1 us (0.78)
  waiting for transfers between devices: 62.5 us -> 38 us
  Pallas kernels: 0 us -> 19.1 us
  starting transfers between devices: 3.28 us -> 18 us
  between operations: 13.5 us -> 0.13 us
  other arithmetic: 9.54 us -> 0.03 us
  matrix products: 6.94 us -> 0 us
  local copies, waits for them, and re-layouts: 6.4 us -> 3.41 us
    all_gather x2 -> x0, waiting for transfers between devices: 37 us -> none  [body(): halves.append(lax.all_gather(local, 'tensor', axis=1, tiled=True))]
    pallas_call x0 -> x10, Pallas kernels: none -> 19.1 us  [the longest x4 11.1 us: attend(): pl.pallas_call(functools.partial(attend_kernel, chunk=chunk, block_len=bl...]
    ppermute x3 -> x18, starting transfers between devices: 3.05 us -> 18 us  [the longest x10 16.9 us: shift(): return lax.ppermute(x, axis, [(i, (i + distance) % n) for i in range(n)])]
    ppermute x3 -> x18, waiting for transfers between devices: 25.5 us -> 38 us  [the longest x10 36.4 us: shift(): return lax.ppermute(x, axis, [(i, (i + distance) % n) for i in range(n)])]
    dot_general x4 -> x0, matrix products: 6.94 us -> none  [the longest x2 4.34 us: attend(): jnp.einsum('grqk,kgd->qgrd', rounded, value_gathered, preferred_element_t...]
    concatenate x2 -> x0, other arithmetic: 4.68 us -> none  [the longest x1 4.67 us: body(): return jnp.concatenate(halves, 0)]
    reduce_sum x2 -> x0, other arithmetic: 3.49 us -> none  [attend(): total = jnp.sum(weights, axis=-1)]
    convert_element_type x2 -> x0, local copies, waits for them, and re-layouts: 2.04 us -> none  [attend(): mixed.reshape(rows, groups * group_factor * HEAD_WIDTH).astype(jnp.bfloat16)]
  transfers between devices with their start and end apart: 5 -> 18, of which waited for: 5 -> 6; matrix products, arithmetic and copies ran while one was open for 10% -> 0% of each run, Pallas kernels for 0% -> 23%
where the time goes in v1:
time: 79.1 us; the launch traced here: 78.7 us
  waiting for transfers between devices  38 us (48%)
  Pallas kernels  19.1 us (24%)
  starting transfers between devices  18 us (23%)
  local copies, waits for them, and re-layouts  3.41 us (4%)
    ppermute x10, waiting for transfers between devices, shift(): return lax.ppermute(x, axis, [(i, (i + distance) % n) for i in range(n)])  36.4 us
    ppermute x10, starting transfers between devices, shift(): return lax.ppermute(x, axis, [(i, (i + distance) % n) for i in range(n)])  16.9 us
    pallas_call x4, Pallas kernels, attend(): pl.pallas_call(functools.partial(attend_kernel, chunk=chunk, block_len=bl...  11.1 us
    pallas_call x5, Pallas kernels, place(): pl.pallas_call(functools.partial(place_kernel, spots=tuple((e[1:] for e i...  5.94 us
    unnamed x8, local copies, waits for them, and re-layouts  2.46 us
    pallas_call x1, Pallas kernels, prepare(): pl.pallas_call(functools.partial(prepare_kernel, chunks=chunks, block_len...  2.14 us
  transfers between devices with their start and end apart: 18, of which 6 were waited for; matrix products, arithmetic and copies ran while one was open for 0% of the time, Pallas kernels for 23%

profile of v1, /device:TPU:0, one launch (start us, length us, event | category | flops | bytes accessed | tf_op | source)
XLA Modules:
  0.0 78.7 jit_solution(13965792670772718544)
XLA Ops:
  0.0 1.0 %slice_bitcast_fusion = (bf16[1,256,128]{2,1,0:T(8,128)(2,1)S(1)}, bf16[1,256,128]{2,1,0:T(8,128)(2,1)S(1)}, bf16[1,256,128]{2,1,0:T(8,128)(2,1)S(1)}, bf16[1,256,128]{2,1,0:T(8,128)(2,1)S(1)}) fusion(bf16[256,256]{1,0:T(8,128)(2,1)} %param.6, bf16[256,256]{1,0:T(8,128)(2,1)} %param.5), kind=kLoop, calls=%fused_computation.2 | loop fusion | bytes 524288 | tf_op jit(solution)/shard_map/stack | solution.py:182
  1.0 4.1 %collective-permute-start.2 = (bf16[2,256,128]{2,1,0:T(8,128)(2,1)S(1)}, bf16[2,256,128]{2,1,0:T(8,128)(2,1)S(1)}, u32[]{:S(2)}, u32[]{:S(2)}) collective-permute-start(bf16[2,256,128]{2,1,0:T(8,128)(2,1)S(1)} %pad_maximum_fusion.rest_0_), channel_id=1, source_target_pairs={{0,12},{4,16},{8,20},{12,24},{16,28},{20,0},{24,4},{28,8},{1,13},{... | collective-permute-start | bytes 393224 | tf_op jit(solution)/shard_map/ppermute | solution.py:26
  5.0 1.6 %collective-permute-start.1 = (bf16[2,256,128]{2,1,0:T(8,128)(2,1)S(1)}, bf16[2,256,128]{2,1,0:T(8,128)(2,1)S(1)}, u32[]{:S(2)}, u32[]{:S(2)}) collective-permute-start(bf16[2,256,128]{2,1,0:T(8,128)(2,1)S(1)} %pad_maximum_fusion.rest_0_), channel_id=1, source_target_pairs={{0,8},{4,12},{8,16},{12,20},{16,24},{20,28},{24,0},{28,4},{1,9},{5... | collective-permute-start | bytes 393224 | tf_op jit(solution)/shard_map/ppermute | solution.py:26
  6.6 1.5 %collective-permute-start = (bf16[2,256,128]{2,1,0:T(8,128)(2,1)S(1)}, bf16[2,256,128]{2,1,0:T(8,128)(2,1)S(1)}, u32[]{:S(2)}, u32[]{:S(2)}) collective-permute-start(bf16[2,256,128]{2,1,0:T(8,128)(2,1)S(1)} %pad_maximum_fusion.rest_0_), channel_id=1, source_target_pairs={{0,4},{4,8},{8,12},{12,16},{16,20},{20,24},{24,28},{28,0},{1,5},{5... | collective-permute-start | bytes 393224 | tf_op jit(solution)/shard_map/ppermute | solution.py:26
  8.2 1.2 %collective-permute-start.7 = (bf16[2,256,128]{2,1,0:T(8,128)(2,1)S(1)}, bf16[2,256,128]{2,1,0:T(8,128)(2,1)}, u32[]{:S(2)}, u32[]{:S(2)}) collective-permute-start(bf16[2,256,128]{2,1,0:T(8,128)(2,1)S(1)} %pad_maximum_fusion.1.rest_0_), channel_id=1, source_target_pairs={{0,12},{4,16},{8,20},{12,24},{16,28},{20,0},{24,4},{28,8},{1,13},{... | collective-permute-start | bytes 393224 | tf_op jit(solution)/shard_map/ppermute | solution.py:26
  9.4 1.6 %collective-permute-start.6 = (bf16[2,256,128]{2,1,0:T(8,128)(2,1)S(1)}, bf16[2,256,128]{2,1,0:T(8,128)(2,1)}, u32[]{:S(2)}, u32[]{:S(2)}) collective-permute-start(bf16[2,256,128]{2,1,0:T(8,128)(2,1)S(1)} %pad_maximum_fusion.1.rest_0_), channel_id=1, source_target_pairs={{0,8},{4,12},{8,16},{12,20},{16,24},{20,28},{24,0},{28,4},{1,9},{5... | collective-permute-start | bytes 393224 | tf_op jit(solution)/shard_map/ppermute | solution.py:26
  11.0 13.5 %collective-permute-done.2.rest_3_ = bf16[2,256,128]{2,1,0:T(8,128)(2,1)S(1)} collective-permute-done((bf16[2,256,128]{2,1,0:T(8,128)(2,1)S(1)}, bf16[2,256,128]{2,1,0:T(8,128)(2,1)S(1)}, u32[]{:S(2)}, u32[]{:S(2)}) %collective-permute-start.2) | collective-permute-done | bytes 131104 | tf_op jit(solution)/shard_map/ppermute | solution.py:26
  24.4 0.0 copy-start
  24.4 0.0 collective-permute-start.5
  24.5 2.1 %prepare.1 = (bf16[4,1024,256]{2,1,0:T(8,128)(2,1)S(1)}, bf16[256,1024]{1,0:T(8,128)(2,1)S(1)}) custom-call(s32[16]{0:T(128)} %pos_ref.1, bf16[256,2048]{1,0:T(8,128)(2,1)} %q_ref.1), custom_call_target="tpu_custom_call" | custom-call | tf_op jit(solution)/shard_map/prepare/pallas_call | solution.py:74
  26.6 0.0 collective-permute-done.1.rest_2_
  26.6 0.0 collective-permute-done.rest_1_
  26.6 0.0 copy-done
  26.6 0.0 copy-start.2
  26.6 0.6 copy-done.2
  27.3 0.0 copy-start.1
  27.3 0.9 %copy-done.1 = bf16[2,256,128]{2,1,0:T(8,128)(2,1)S(1)} copy-done((bf16[2,256,128]{2,1,0:T(8,128)(2,1)S(1)}, bf16[2,256,128]{2,1,0:T(8,128)(2,1)}, u32[]{:S(2)}) %copy-start.1) | copy-done | bytes 131096
  28.2 0.0 copy-start.3
  28.2 0.9 %copy-done.3 = bf16[2,256,128]{2,1,0:T(8,128)(2,1)S(1)} copy-done((bf16[2,256,128]{2,1,0:T(8,128)(2,1)S(1)}, bf16[2,256,128]{2,1,0:T(8,128)(2,1)}, u32[]{:S(2)}) %copy-start.3) | copy-done | bytes 131096
  29.1 2.4 %shard_map.46.refs_6_ = bf16[128,1024]{1,0:T(8,128)(2,1)} custom-call(bf16[4,1024,256]{2,1,0:T(8,128)(2,1)S(1)} %get-tuple-element.15.stack_ref, bf16[256,1024]{1,0:T(8,128)(2,1)S(1)} %get-tuple-element.16.mask_ref, bf16[2,256,128]{2,1,0:T(8,128)(2,1)S(1)} %pad_maximum_fusion.rest_0_, bf16[2,256,128]{2,1,0:T(8,128)(2,1)S(1)} %copy-done.3, ...), custom_call_target="tpu_custom_call" | custom-call | tf_op jit(solution)/shard_map/pallas_call | solution.py:126
  31.5 0.0 collective-permute-start.13
  31.5 2.4 %shard_map.47.refs_4_ = bf16[128,1024]{1,0:T(8,128)(2,1)} custom-call(bf16[4,1024,256]{2,1,0:T(8,128)(2,1)S(1)} %get-tuple-element.15.stack_ref, bf16[256,1024]{1,0:T(8,128)(2,1)S(1)} %get-tuple-element.16.mask_ref, bf16[2,256,128]{2,1,0:T(8,128)(2,1)S(1)} %pad_maximum_fusion.rest_0_, bf16[2,256,128]{2,1,0:T(8,128)(2,1)S(1)} %copy-done.3, ...), custom_call_target="tpu_custom_call" | custom-call | tf_op jit(solution)/shard_map/pallas_call | solution.py:126
  33.9 0.5 collective-permute-start.12
  34.5 0.0 collective-permute-done.7.rest_3_
  34.5 0.0 collective-permute-done.6.rest_2_
  34.5 0.0 collective-permute-done.5.rest_1_
  34.5 3.5 %shard_map.48.refs_2_ = bf16[128,1024]{1,0:T(8,128)(2,1)} custom-call(bf16[4,1024,256]{2,1,0:T(8,128)(2,1)S(1)} %get-tuple-element.15.stack_ref, bf16[256,1024]{1,0:T(8,128)(2,1)S(1)} %get-tuple-element.16.mask_ref, bf16[2,256,128]{2,1,0:T(8,128)(2,1)S(1)} %pad_maximum_fusion.1.rest_0_, bf16[2,256,128]{2,1,0:T(8,128)(2,1)} %collective-permute-done.5.rest_1_, ...), custom_call_target="tpu_custom_call" | custom-call | tf_op jit(solution)/shard_map/pallas_call | solution.py:126
  37.9 0.0 collective-permute-start.11
  37.9 2.8 %shard_map.49.refs_0_ = bf16[128,1024]{1,0:T(8,128)(2,1)S(1)} custom-call(bf16[4,1024,256]{2,1,0:T(8,128)(2,1)S(1)} %get-tuple-element.15.stack_ref, bf16[256,1024]{1,0:T(8,128)(2,1)S(1)} %get-tuple-element.16.mask_ref, bf16[2,256,128]{2,1,0:T(8,128)(2,1)S(1)} %pad_maximum_fusion.1.rest_0_, bf16[2,256,128]{2,1,0:T(8,128)(2,1)} %collective-permute-done.5.rest_1_, ...), custom_call_target="tpu_custom_call" | custom-call | tf_op jit(solution)/shard_map/pallas_call | solution.py:126
  40.7 0.6 collective-permute-start.10
  41.3 1.7 %collective-permute-start.9 = (bf16[128,1024]{1,0:T(8,128)(2,1)S(1)}, bf16[128,1024]{1,0:T(8,128)(2,1)S(1)}, u32[]{:S(2)}, u32[]{:S(2)}) collective-permute-start(bf16[128,1024]{1,0:T(8,128)(2,1)S(1)} %shard_map.49.refs_0_), channel_id=1, source_target_pairs={{0,2},{1,3},{2,0},{3,1},{4,6},{5,7},{6,4},{7,5},{8,10},{9,11},{10,... | collective-permute-start | bytes 786440 | tf_op jit(solution)/shard_map/ppermute | solution.py:26
  43.0 0.0 collective-permute-done.13.refs_7_
  43.0 0.0 collective-permute-done.12.refs_5_
  43.0 0.0 collective-permute-done.11.refs_3_
  43.0 0.0 collective-permute-done.10.refs_1_
  43.0 2.7 %place.5.refs_2_ = bf16[256,8192]{1,0:T(8,128)(2,1)} custom-call(bf16[128,1024]{1,0:T(8,128)(2,1)S(1)} %shard_map.49.refs_0_, bf16[128,1024]{1,0:T(8,128)(2,1)S(1)} %collective-permute-done.10.refs_1_, bf16[128,1024]{1,0:T(8,128)(2,1)} %shard_map.48.refs_2_, bf16[128,1024]{1,0:T(8,128)(2,1)} %collective-permute-done.11.refs_3_, ...), custom_call_target="tpu_custom_call" | custom-call | tf_op jit(solution)/shard_map/place/pallas_call | solution.py:160
  45.7 3.8 %collective-permute-done.9.refs_0_ = bf16[128,1024]{1,0:T(8,128)(2,1)S(1)} collective-permute-done((bf16[128,1024]{1,0:T(8,128)(2,1)S(1)}, bf16[128,1024]{1,0:T(8,128)(2,1)S(1)}, u32[]{:S(2)}, u32[]{:S(2)}) %collective-permute-start.9) | collective-permute-done | bytes 262176 | tf_op jit(solution)/shard_map/ppermute | solution.py:26
  49.5 0.0 collective-permute-start.14
  49.5 1.7 %collective-permute-start.8 = (bf16[128,1024]{1,0:T(8,128)(2,1)}, bf16[128,1024]{1,0:T(8,128)(2,1)S(1)}, u32[]{:S(2)}, u32[]{:S(2)}) collective-permute-start(bf16[128,1024]{1,0:T(8,128)(2,1)} %shard_map.48.refs_2_), channel_id=1, source_target_pairs={{0,2},{1,3},{2,0},{3,1},{4,6},{5,7},{6,4},{7,5},{8,10},{9,11},{10,... | collective-permute-start | bytes 786440 | tf_op jit(solution)/shard_map/ppermute | solution.py:26
  51.3 0.0 collective-permute-done.14.refs_1_
  51.3 0.8 %place.6.refs_2_ = bf16[256,8192]{1,0:T(8,128)(2,1)} custom-call(bf16[128,1024]{1,0:T(8,128)(2,1)S(1)} %collective-permute-done.9.refs_0_, bf16[128,1024]{1,0:T(8,128)(2,1)S(1)} %collective-permute-done.14.refs_1_, bf16[256,8192]{1,0:T(8,128)(2,1)} %place.5.refs_2_), custom_call_target="tpu_custom_call", output_to_operand_aliasing={{}: (2, {})} | custom-call | tf_op jit(solution)/shard_map/place/pallas_call | solution.py:160
  52.1 6.4 %collective-permute-done.8.refs_0_ = bf16[128,1024]{1,0:T(8,128)(2,1)S(1)} collective-permute-done((bf16[128,1024]{1,0:T(8,128)(2,1)}, bf16[128,1024]{1,0:T(8,128)(2,1)S(1)}, u32[]{:S(2)}, u32[]{:S(2)}) %collective-permute-start.8) | collective-permute-done | bytes 262176 | tf_op jit(solution)/shard_map/ppermute | solution.py:26
  58.5 0.0 collective-permute-start.15
  58.5 1.7 %collective-permute-start.4 = (bf16[128,1024]{1,0:T(8,128)(2,1)}, bf16[128,1024]{1,0:T(8,128)(2,1)S(1)}, u32[]{:S(2)}, u32[]{:S(2)}) collective-permute-start(bf16[128,1024]{1,0:T(8,128)(2,1)} %shard_map.47.refs_4_), channel_id=1, source_target_pairs={{0,2},{1,3},{2,0},{3,1},{4,6},{5,7},{6,4},{7,5},{8,10},{9,11},{10,... | collective-permute-start | bytes 786440 | tf_op jit(solution)/shard_map/ppermute | solution.py:26
  60.2 0.0 collective-permute-done.15.refs_1_
  60.2 0.8 %place.7.refs_2_ = bf16[256,8192]{1,0:T(8,128)(2,1)} custom-call(bf16[128,1024]{1,0:T(8,128)(2,1)S(1)} %collective-permute-done.8.refs_0_, bf16[128,1024]{1,0:T(8,128)(2,1)S(1)} %collective-permute-done.15.refs_1_, bf16[256,8192]{1,0:T(8,128)(2,1)} %place.6.refs_2_), custom_call_target="tpu_custom_call", output_to_operand_aliasing={{}: (2, {})} | custom-call | tf_op jit(solution)/shard_map/place/pallas_call | solution.py:160
  61.0 6.4 %collective-permute-done.4.refs_0_ = bf16[128,1024]{1,0:T(8,128)(2,1)S(1)} collective-permute-done((bf16[128,1024]{1,0:T(8,128)(2,1)}, bf16[128,1024]{1,0:T(8,128)(2,1)S(1)}, u32[]{:S(2)}, u32[]{:S(2)}) %collective-permute-start.4) | collective-permute-done | bytes 262176 | tf_op jit(solution)/shard_map/ppermute | solution.py:26
  67.4 0.0 collective-permute-start.16
  67.4 1.7 %collective-permute-start.3 = (bf16[128,1024]{1,0:T(8,128)(2,1)}, bf16[128,1024]{1,0:T(8,128)(2,1)S(1)}, u32[]{:S(2)}, u32[]{:S(2)}) collective-permute-start(bf16[128,1024]{1,0:T(8,128)(2,1)} %shard_map.46.refs_6_), channel_id=1, source_target_pairs={{0,2},{1,3},{2,0},{3,1},{4,6},{5,7},{6,4},{7,5},{8,10},{9,11},{10,... | collective-permute-start | bytes 786440 | tf_op jit(solution)/shard_map/ppermute | solution.py:26
  69.1 0.0 collective-permute-done.16.refs_1_
  69.2 0.8 %place.8.refs_2_ = bf16[256,8192]{1,0:T(8,128)(2,1)} custom-call(bf16[128,1024]{1,0:T(8,128)(2,1)S(1)} %collective-permute-done.4.refs_0_, bf16[128,1024]{1,0:T(8,128)(2,1)S(1)} %collective-permute-done.16.refs_1_, bf16[256,8192]{1,0:T(8,128)(2,1)} %place.7.refs_2_), custom_call_target="tpu_custom_call", output_to_operand_aliasing={{}: (2, {})} | custom-call | tf_op jit(solution)/shard_map/place/pallas_call | solution.py:160
  70.0 6.4 %collective-permute-done.3.refs_0_ = bf16[128,1024]{1,0:T(8,128)(2,1)S(1)} collective-permute-done((bf16[128,1024]{1,0:T(8,128)(2,1)}, bf16[128,1024]{1,0:T(8,128)(2,1)S(1)}, u32[]{:S(2)}, u32[]{:S(2)}) %collective-permute-start.3) | collective-permute-done | bytes 262176 | tf_op jit(solution)/shard_map/ppermute | solution.py:26
  76.3 0.0 collective-permute-start.17
  76.3 1.5 %collective-permute-done.17.refs_1_ = bf16[128,1024]{1,0:T(8,128)(2,1)S(1)} collective-permute-done((bf16[128,1024]{1,0:T(8,128)(2,1)S(1)}, bf16[128,1024]{1,0:T(8,128)(2,1)S(1)}, u32[]{:S(2)}, u32[]{:S(2)}) %collective-permute-start.17) | collective-permute-done | bytes 262176 | tf_op jit(solution)/shard_map/ppermute | solution.py:31
  77.9 0.8 %place.9 = bf16[256,8192]{1,0:T(8,128)(2,1)} custom-call(bf16[128,1024]{1,0:T(8,128)(2,1)S(1)} %collective-permute-done.3.refs_0_, bf16[128,1024]{1,0:T(8,128)(2,1)S(1)} %collective-permute-done.17.refs_1_, bf16[256,8192]{1,0:T(8,128)(2,1)} %place.8.refs_2_), custom_call_target="tpu_custom_call", output_to_operand_aliasing={{}: (2, {})} | custom-call | tf_op jit(solution)/shard_map/place/pallas_call | solution.py:160
  (2 shorter events, 0.0 us)
Async XLA Ops:
  1.0 23.5 %collective-permute-start.2 = (bf16[2,256,128]{2,1,0:T(8,128)(2,1)S(1)}, bf16[2,256,128]{2,1,0:T(8,128)(2,1)S(1)}, u32[]{:S(2)}, u32[]{:S(2)}) collective-permute-start(bf16[2,256,128]{2,1,0:T(8,128)(2,1)S(1)} %pad_maximum_fusion.rest_0_), channel_id=1, source_target_pairs={{0,12},{4,16},{8,20},{12,24},{16,28},{20,0},{24,4},{28,8},{1,13},{... | collective-permute-start | bytes 393224 | tf_op jit(solution)/shard_map/ppermute | solution.py:26
  5.0 21.6 %collective-permute-start.1 = (bf16[2,256,128]{2,1,0:T(8,128)(2,1)S(1)}, bf16[2,256,128]{2,1,0:T(8,128)(2,1)S(1)}, u32[]{:S(2)}, u32[]{:S(2)}) collective-permute-start(bf16[2,256,128]{2,1,0:T(8,128)(2,1)S(1)} %pad_maximum_fusion.rest_0_), channel_id=1, source_target_pairs={{0,8},{4,12},{8,16},{12,20},{16,24},{20,28},{24,0},{28,4},{1,9},{5... | collective-permute-start | bytes 393224 | tf_op jit(solution)/shard_map/ppermute | solution.py:26
  6.6 20.0 %collective-permute-start = (bf16[2,256,128]{2,1,0:T(8,128)(2,1)S(1)}, bf16[2,256,128]{2,1,0:T(8,128)(2,1)S(1)}, u32[]{:S(2)}, u32[]{:S(2)}) collective-permute-start(bf16[2,256,128]{2,1,0:T(8,128)(2,1)S(1)} %pad_maximum_fusion.rest_0_), channel_id=1, source_target_pairs={{0,4},{4,8},{8,12},{12,16},{16,20},{20,24},{24,28},{28,0},{1,5},{5... | collective-permute-start | bytes 393224 | tf_op jit(solution)/shard_map/ppermute | solution.py:26
  8.2 26.3 %collective-permute-start.7 = (bf16[2,256,128]{2,1,0:T(8,128)(2,1)S(1)}, bf16[2,256,128]{2,1,0:T(8,128)(2,1)}, u32[]{:S(2)}, u32[]{:S(2)}) collective-permute-start(bf16[2,256,128]{2,1,0:T(8,128)(2,1)S(1)} %pad_maximum_fusion.1.rest_0_), channel_id=1, source_target_pairs={{0,12},{4,16},{8,20},{12,24},{16,28},{20,0},{24,4},{28,8},{1,13},{... | collective-permute-start | bytes 393224 | tf_op jit(solution)/shard_map/ppermute | solution.py:26
  9.4 25.1 %collective-permute-start.6 = (bf16[2,256,128]{2,1,0:T(8,128)(2,1)S(1)}, bf16[2,256,128]{2,1,0:T(8,128)(2,1)}, u32[]{:S(2)}, u32[]{:S(2)}) collective-permute-start(bf16[2,256,128]{2,1,0:T(8,128)(2,1)S(1)} %pad_maximum_fusion.1.rest_0_), channel_id=1, source_target_pairs={{0,8},{4,12},{8,16},{12,20},{16,24},{20,28},{24,0},{28,4},{1,9},{5... | collective-permute-start | bytes 393224 | tf_op jit(solution)/shard_map/ppermute | solution.py:26
  24.4 2.2 %copy-start = (bf16[2,256,128]{2,1,0:T(8,128)(2,1)}, bf16[2,256,128]{2,1,0:T(8,128)(2,1)S(1)}, u32[]{:S(2)}) copy-start(bf16[2,256,128]{2,1,0:T(8,128)(2,1)S(1)} %collective-permute-done.2.rest_3_) | copy-start | bytes 393220
  24.4 10.0 %collective-permute-start.5 = (bf16[2,256,128]{2,1,0:T(8,128)(2,1)S(1)}, bf16[2,256,128]{2,1,0:T(8,128)(2,1)}, u32[]{:S(2)}, u32[]{:S(2)}) collective-permute-start(bf16[2,256,128]{2,1,0:T(8,128)(2,1)S(1)} %pad_maximum_fusion.1.rest_0_), channel_id=1, source_target_pairs={{0,4},{4,8},{8,12},{12,16},{16,20},{20,24},{24,28},{28,0},{1,5},{5... | collective-permute-start | bytes 393224 | tf_op jit(solution)/shard_map/ppermute | solution.py:26
  26.6 0.7 copy-start.2
  27.3 0.9 %copy-start.1 = (bf16[2,256,128]{2,1,0:T(8,128)(2,1)S(1)}, bf16[2,256,128]{2,1,0:T(8,128)(2,1)}, u32[]{:S(2)}) copy-start(bf16[2,256,128]{2,1,0:T(8,128)(2,1)} %copy-done) | copy-start | bytes 393220
  28.2 0.9 %copy-start.3 = (bf16[2,256,128]{2,1,0:T(8,128)(2,1)S(1)}, bf16[2,256,128]{2,1,0:T(8,128)(2,1)}, u32[]{:S(2)}) copy-start(bf16[2,256,128]{2,1,0:T(8,128)(2,1)} %copy-done.2) | copy-start | bytes 393220
  31.5 11.5 %collective-permute-start.13 = (bf16[128,1024]{1,0:T(8,128)(2,1)}, bf16[128,1024]{1,0:T(8,128)(2,1)}, u32[]{:S(2)}, u32[]{:S(2)}) collective-permute-start(bf16[128,1024]{1,0:T(8,128)(2,1)} %shard_map.46.refs_6_), channel_id=1, source_target_pairs={{0,1},{1,0},{2,3},{3,2},{4,5},{5,4},{6,7},{7,6},{8,9},{9,8},{10,11... | collective-permute-start | bytes 786440 | tf_op jit(solution)/shard_map/ppermute | solution.py:31
  33.9 9.0 %collective-permute-start.12 = (bf16[128,1024]{1,0:T(8,128)(2,1)}, bf16[128,1024]{1,0:T(8,128)(2,1)}, u32[]{:S(2)}, u32[]{:S(2)}) collective-permute-start(bf16[128,1024]{1,0:T(8,128)(2,1)} %shard_map.47.refs_4_), channel_id=1, source_target_pairs={{0,1},{1,0},{2,3},{3,2},{4,5},{5,4},{6,7},{7,6},{8,9},{9,8},{10,11... | collective-permute-start | bytes 786440 | tf_op jit(solution)/shard_map/ppermute | solution.py:31
  37.9 5.1 %collective-permute-start.11 = (bf16[128,1024]{1,0:T(8,128)(2,1)}, bf16[128,1024]{1,0:T(8,128)(2,1)}, u32[]{:S(2)}, u32[]{:S(2)}) collective-permute-start(bf16[128,1024]{1,0:T(8,128)(2,1)} %shard_map.48.refs_2_), channel_id=1, source_target_pairs={{0,1},{1,0},{2,3},{3,2},{4,5},{5,4},{6,7},{7,6},{8,9},{9,8},{10,11... | collective-permute-start | bytes 786440 | tf_op jit(solution)/shard_map/ppermute | solution.py:31
  40.7 2.3 %collective-permute-start.10 = (bf16[128,1024]{1,0:T(8,128)(2,1)S(1)}, bf16[128,1024]{1,0:T(8,128)(2,1)S(1)}, u32[]{:S(2)}, u32[]{:S(2)}) collective-permute-start(bf16[128,1024]{1,0:T(8,128)(2,1)S(1)} %shard_map.49.refs_0_), channel_id=1, source_target_pairs={{0,1},{1,0},{2,3},{3,2},{4,5},{5,4},{6,7},{7,6},{8,9},{9,8},{10,11... | collective-permute-start | bytes 786440 | tf_op jit(solution)/shard_map/ppermute | solution.py:31
  41.3 8.3 %collective-permute-start.9 = (bf16[128,1024]{1,0:T(8,128)(2,1)S(1)}, bf16[128,1024]{1,0:T(8,128)(2,1)S(1)}, u32[]{:S(2)}, u32[]{:S(2)}) collective-permute-start(bf16[128,1024]{1,0:T(8,128)(2,1)S(1)} %shard_map.49.refs_0_), channel_id=1, source_target_pairs={{0,2},{1,3},{2,0},{3,1},{4,6},{5,7},{6,4},{7,5},{8,10},{9,11},{10,... | collective-permute-start | bytes 786440 | tf_op jit(solution)/shard_map/ppermute | solution.py:26
  49.5 1.7 %collective-permute-start.14 = (bf16[128,1024]{1,0:T(8,128)(2,1)S(1)}, bf16[128,1024]{1,0:T(8,128)(2,1)S(1)}, u32[]{:S(2)}, u32[]{:S(2)}) collective-permute-start(bf16[128,1024]{1,0:T(8,128)(2,1)S(1)} %collective-permute-done.9.refs_0_), channel_id=1, source_target_pairs={{0,1},{1,0},{2,3},{3,2},{4,5},{5,4},{6,7},{7,6},{8,9},{9,8},{10,11... | collective-permute-start | bytes 786440 | tf_op jit(solution)/shard_map/ppermute | solution.py:31
  49.5 8.9 %collective-permute-start.8 = (bf16[128,1024]{1,0:T(8,128)(2,1)}, bf16[128,1024]{1,0:T(8,128)(2,1)S(1)}, u32[]{:S(2)}, u32[]{:S(2)}) collective-permute-start(bf16[128,1024]{1,0:T(8,128)(2,1)} %shard_map.48.refs_2_), channel_id=1, source_target_pairs={{0,2},{1,3},{2,0},{3,1},{4,6},{5,7},{6,4},{7,5},{8,10},{9,11},{10,... | collective-permute-start | bytes 786440 | tf_op jit(solution)/shard_map/ppermute | solution.py:26
  58.5 1.7 %collective-permute-start.15 = (bf16[128,1024]{1,0:T(8,128)(2,1)S(1)}, bf16[128,1024]{1,0:T(8,128)(2,1)S(1)}, u32[]{:S(2)}, u32[]{:S(2)}) collective-permute-start(bf16[128,1024]{1,0:T(8,128)(2,1)S(1)} %collective-permute-done.8.refs_0_), channel_id=1, source_target_pairs={{0,1},{1,0},{2,3},{3,2},{4,5},{5,4},{6,7},{7,6},{8,9},{9,8},{10,11... | collective-permute-start | bytes 786440 | tf_op jit(solution)/shard_map/ppermute | solution.py:31
  58.5 8.9 %collective-permute-start.4 = (bf16[128,1024]{1,0:T(8,128)(2,1)}, bf16[128,1024]{1,0:T(8,128)(2,1)S(1)}, u32[]{:S(2)}, u32[]{:S(2)}) collective-permute-start(bf16[128,1024]{1,0:T(8,128)(2,1)} %shard_map.47.refs_4_), channel_id=1, source_target_pairs={{0,2},{1,3},{2,0},{3,1},{4,6},{5,7},{6,4},{7,5},{8,10},{9,11},{10,... | collective-permute-start | bytes 786440 | tf_op jit(solution)/shard_map/ppermute | solution.py:26
  67.4 1.7 %collective-permute-start.16 = (bf16[128,1024]{1,0:T(8,128)(2,1)S(1)}, bf16[128,1024]{1,0:T(8,128)(2,1)S(1)}, u32[]{:S(2)}, u32[]{:S(2)}) collective-permute-start(bf16[128,1024]{1,0:T(8,128)(2,1)S(1)} %collective-permute-done.4.refs_0_), channel_id=1, source_target_pairs={{0,1},{1,0},{2,3},{3,2},{4,5},{5,4},{6,7},{7,6},{8,9},{9,8},{10,11... | collective-permute-start | bytes 786440 | tf_op jit(solution)/shard_map/ppermute | solution.py:31
  67.4 8.9 %collective-permute-start.3 = (bf16[128,1024]{1,0:T(8,128)(2,1)}, bf16[128,1024]{1,0:T(8,128)(2,1)S(1)}, u32[]{:S(2)}, u32[]{:S(2)}) collective-permute-start(bf16[128,1024]{1,0:T(8,128)(2,1)} %shard_map.46.refs_6_), channel_id=1, source_target_pairs={{0,2},{1,3},{2,0},{3,1},{4,6},{5,7},{6,4},{7,5},{8,10},{9,11},{10,... | collective-permute-start | bytes 786440 | tf_op jit(solution)/shard_map/ppermute | solution.py:26
  76.3 1.5 %collective-permute-start.17 = (bf16[128,1024]{1,0:T(8,128)(2,1)S(1)}, bf16[128,1024]{1,0:T(8,128)(2,1)S(1)}, u32[]{:S(2)}, u32[]{:S(2)}) collective-permute-start(bf16[128,1024]{1,0:T(8,128)(2,1)S(1)} %collective-permute-done.3.refs_0_), channel_id=1, source_target_pairs={{0,1},{1,0},{2,3},{3,2},{4,5},{5,4},{6,7},{7,6},{8,9},{9,8},{10,11... | collective-permute-start | bytes 786440 | tf_op jit(solution)/shard_map/ppermute | solution.py:31

commit v2 on v1

--- a/solution.py
+++ b/solution.py
@@ -35,72 +35,93 @@
     return pltpu.with_memory_space_constraint(x, pltpu.VMEM)
 
 
-def prepare_kernel(pos_ref, q_ref, stack_ref, mask_ref, sems, *, chunks, block_len, count):
-    copies = []
-    for c in range(chunks):
-        g, qb = c // 2, c % 2
-        for h in range(GROUP):
-            col = (g * GROUP + h) * HEAD_WIDTH
-            copies.append(pltpu.make_async_copy(
-                q_ref.at[qb * block_len:(qb + 1) * block_len, col:col + HEAD_WIDTH],
-                stack_ref.at[c, h * block_len:(h + 1) * block_len, :HEAD_WIDTH],
-                sems.at[c * GROUP + h]))
-    for copy in copies:
-        copy.start()
+def build_mask(pos_ref, mask_ref, block_len, count):
     ahead = (lax.broadcasted_iota(jnp.int32, (block_len, block_len), 1)
              - lax.broadcasted_iota(jnp.int32, (block_len, block_len), 0))
-    unit = jnp.where(ahead == 0, 1.0, 0.0).astype(jnp.bfloat16)
-    for c in range(chunks):
-        for h in range(GROUP):
-            stack_ref[c, h * block_len:(h + 1) * block_len, HEAD_WIDTH:] = unit
     shard = lax.axis_index("seq").astype(jnp.int32)
+    odd = lax.rem(shard, 2)
+    backs = (0, 2, 1 + 2 * odd, 3 - 2 * odd)
     for qb in range(2):
         q_block = pos_ref[2 * shard + qb]
-        for back in range(VISIBLE_SHARDS):
+        for slot, back in enumerate(backs):
             source = lax.rem(shard - back + count, count)
             for kb in range(2):
                 gap = (pos_ref[2 * source + kb] - q_block) * block_len
-                at = (2 * back + kb) * block_len
+                at = (2 * slot + kb) * block_len
                 mask_ref[qb * block_len:(qb + 1) * block_len, at:at + block_len] = jnp.where(
                     ahead + gap <= 0, 0.0, -1e30).astype(jnp.bfloat16)
+
+
+def prepare_kernel(pos_ref, q_ref, *rest, group, block_len, count):
+    stacks = rest[:2]
+    sems = rest[-1]
+    copies = []
+    for qb in range(2):
+        for h in range(GROUP):
+            col = (group * GROUP + h) * HEAD_WIDTH
+            copies.append(pltpu.make_async_copy(
+                q_ref.at[qb * block_len:(qb + 1) * block_len, col:col + HEAD_WIDTH],
+                stacks[qb].at[h * block_len:(h + 1) * block_len],
+                sems.at[qb * GROUP + h]))
+    for copy in copies:
+        copy.start()
+    if group == 0:
+        build_mask(pos_ref, rest[2], block_len, count)
     for copy in copies:
         copy.wait()
 
 
-def prepare(block_pos, queries, groups):
+def prepare(block_pos, queries, group):
     tok = queries.shape[0]
     block_len = tok // 2
-    chunks = 2 * groups
+    masks = 1 if group == 0 else 0
     return pl.pallas_call(
-        functools.partial(prepare_kernel, chunks=chunks, block_len=block_len,
+        functools.partial(prepare_kernel, group=group, block_len=block_len,
                           count=lax.axis_size("seq")),
         in_specs=[SMEM, ANY],
-        out_specs=[LOCAL, LOCAL],
-        out_shape=[
-            pltpu.VMEM((chunks, GROUP * block_len, HEAD_WIDTH + block_len), jnp.bfloat16),
-            pltpu.VMEM((tok, VISIBLE_SHARDS * tok), jnp.bfloat16),
-        ],
-        scratch_shapes=[pltpu.SemaphoreType.DMA((chunks * GROUP,))],
-        name="prepare",
+        out_specs=[LOCAL] * (2 + masks),
+        out_shape=[pltpu.VMEM((GROUP * block_len, HEAD_WIDTH), jnp.bfloat16)] * 2
+        + [pltpu.VMEM((tok, VISIBLE_SHARDS * tok), jnp.bfloat16)] * masks,
+        scratch_shapes=[pltpu.SemaphoreType.DMA((2 * GROUP,))],
     )(block_pos, queries)
 
 
 def attend_kernel(stack_ref, mask_ref, *rest, chunk, block_len):
-    pieces = rest[:VISIBLE_SHARDS]
-    out_ref, k_scr, v_scr = rest[VISIBLE_SHARDS:]
+    own_ref, two_ref, swap_ref, pair_ref, far_ref, out_ref, k_scr, v_scr, q_scr = rest
     tok = 2 * block_len
     qb = chunk % 2
-    for slot, ref in enumerate(pieces):
+
+    def fill(slot, ref):
         k_scr[:HEAD_WIDTH, slot * tok:(slot + 1) * tok] = ref[0].T
         v_scr[slot * tok:(slot + 1) * tok, :HEAD_WIDTH] = ref[1]
+
+    fill(0, own_ref)
+    fill(1, two_ref)
+    fill(2, swap_ref)
+    odd = lax.rem(lax.axis_index("seq").astype(jnp.int32), 2)
+
+    @pl.when(odd == 1)
+    def _():
+        fill(3, pair_ref)
+
+    @pl.when(odd == 0)
+    def _():
+        fill(3, far_ref)
+
     v_scr[:, HEAD_WIDTH:] = jnp.ones((VISIBLE_SHARDS * tok, HEAD_WIDTH), jnp.bfloat16)
     k_scr[HEAD_WIDTH:, :] = mask_ref[qb * block_len:(qb + 1) * block_len, :]
+    unit = jnp.where(lax.broadcasted_iota(jnp.int32, (block_len, block_len), 1)
+                     == lax.broadcasted_iota(jnp.int32, (block_len, block_len), 0),
+                     1.0, 0.0).astype(jnp.bfloat16)
+    q_scr[:, :HEAD_WIDTH] = stack_ref[...]
+    for h in range(GROUP):
+        q_scr[h * block_len:(h + 1) * block_len, HEAD_WIDTH:] = unit
     scale = math.log2(math.e) / math.sqrt(HEAD_WIDTH)
     tile = TILE_HEADS * block_len
     steps = GROUP // TILE_HEADS
 
     def scores(t):
-        q = stack_ref[chunk, t * tile:(t + 1) * tile, :]
+        q = q_scr[t * tile:(t + 1) * tile, :]
         return jnp.dot(q, k_scr[...], preferred_element_type=jnp.float32)
 
     def finish(t, s):
@@ -125,12 +146,13 @@
     seen = mask.shape[1]
     return pl.pallas_call(
         functools.partial(attend_kernel, chunk=chunk, block_len=block_len),
-        in_specs=[LOCAL] * (2 + VISIBLE_SHARDS),
+        in_specs=[LOCAL] * (2 + len(pieces)),
         out_specs=LOCAL,
         out_shape=pltpu.VMEM((block_len, GROUP * HEAD_WIDTH), jnp.bfloat16),
         scratch_shapes=[
             pltpu.VMEM((HEAD_WIDTH + block_len, seen), jnp.bfloat16),
             pltpu.VMEM((seen, 2 * HEAD_WIDTH), jnp.bfloat16),
+            pltpu.VMEM((GROUP * block_len, HEAD_WIDTH + block_len), jnp.bfloat16),
         ],
     )(resident(stack), resident(mask), *[resident(p) for p in pieces])
 
@@ -174,37 +196,57 @@
     block_len = tok // 2
     groups = keys.shape[1] // HEAD_WIDTH
     tensor = lax.axis_size("tensor")
+    count = lax.axis_size("seq")
     shape = (tok, queries.shape[1] * tensor)
 
     pieces = []
     for g in range(groups):
         at = slice(g * HEAD_WIDTH, (g + 1) * HEAD_WIDTH)
         own = jnp.stack([keys[:, at], values[:, at]])
-        behind = [own]
-        for back in range(1, VISIBLE_SHARDS):
-            behind.append(shift(own, "seq", back))
-        pieces.append(behind)
-    stack, mask = prepare(block_pos, queries, groups)
+        pair = partner(own, "seq")
+        two = shift(own, "seq", 2)
+        swap = partner(two, "seq")
+        far = lax.ppermute(pair, "seq", [(i, (i + 4) % count) for i in range(0, count, 2)])
+        pieces.append((own, two, swap, pair, far))
+    *stacks, mask = prepare(block_pos, queries, 0)
+    for g in range(1, groups):
+        stacks += prepare(block_pos, queries, g)
 
     arrivals = []
     beside = []
     for chunk in range(2 * groups):
         g, qb = chunk // 2, chunk % 2
         row = qb * block_len
-        local = attend(stack, mask, chunk, pieces[g])
+        local = attend(stacks[chunk], mask, chunk, pieces[g])
         now = []
         for hop in range(1, tensor // 2):
             now.append((shift(local, "tensor", 2 * hop), row, hop, False, g))
         arrivals.append(now)
         beside.append((local, row, 0, False, g))
         beside.append((partner(local, "tensor"), row, 0, True, g))
-    out = place(None, shape, groups, beside)
-    for now in arrivals:
+
+    def crossed(chunk):
+        return [(partner(e[0], "tensor"),) + e[1:3] + (True,) + e[4:]
+                for e in arrivals[chunk]]
+
+    early = 2 * groups - 2
+    out = None
+    if early:
+        out = place(None, shape, groups, beside[:2 * early])
+    batch = beside[2 * early:]
+    if early:
+        batch = batch + arrivals[0] + crossed(0)
+    out = place(out, shape, groups, batch)
+    held = []
+    for chunk in range(1 if early else 0, 2 * groups):
+        now = arrivals[chunk]
         if now:
             first, out = lax.optimization_barrier((now[0][0], out))
             now[0] = (first,) + now[0][1:]
-            crossed = [(partner(e[0], "tensor"),) + e[1:3] + (True,) + e[4:] for e in now]
-            out = place(out, shape, groups, now + crossed)
+            held = held + now + crossed(chunk)
+            if chunk >= early:
+                out = place(out, shape, groups, held)
+                held = []
     return out
 
 

time: 79.1 us -> 68.9 us (0.87)
  waiting for transfers between devices: 38 us -> 31.4 us
  Pallas kernels: 19.1 us -> 16 us
  local copies, waits for them, and re-layouts: 3.41 us -> 2.59 us
    ppermute x10 -> x6, waiting for transfers between devices: 36.4 us -> 18.9 us  [shift(): return lax.ppermute(x, axis, [(i, (i + distance) % n) for i in range(n)])]
    ppermute x0 -> x2, waiting for transfers between devices: none -> 9.11 us  [body(): lax.ppermute(pair, 'seq', [(i, (i + 4) % count) for i in range(0, count,...]
    ppermute x10 -> x6, starting transfers between devices: 16.9 us -> 8.86 us  [shift(): return lax.ppermute(x, axis, [(i, (i + distance) % n) for i in range(n)])]
    ppermute x0 -> x2, starting transfers between devices: none -> 4.55 us  [body(): lax.ppermute(pair, 'seq', [(i, (i + 4) % count) for i in range(0, count,...]
    ppermute x8 -> x12, starting transfers between devices: 1.09 us -> 4.84 us  [partner(): return lax.ppermute(x, axis, [(i, i ^ 1) for i in range(n)])]
    pallas_call x4, Pallas kernels: 11.1 us -> 7.44 us  [attend(): pl.pallas_call(functools.partial(attend_kernel, chunk=chunk, block_len=bl...]
    ppermute x8 -> x12, waiting for transfers between devices: 1.55 us -> 3.44 us  [partner(): return lax.ppermute(x, axis, [(i, i ^ 1) for i in range(n)])]
    pallas_call x1 -> x2, Pallas kernels: 2.14 us -> 3.63 us  [prepare(): pl.pallas_call(functools.partial(prepare_kernel, group=group, block_len=b...]
  transfers between devices with their start and end apart: 18 -> 20, of which waited for: 6 -> 10; matrix products, arithmetic and copies ran while one was open for 0% -> 0% of each run, Pallas kernels for 23% -> 22%
where the time goes in v2:
time: 68.9 us; the launch traced here: 68.5 us
  waiting for transfers between devices  31.4 us (46%)
  starting transfers between devices  18.2 us (26%)
  Pallas kernels  16 us (23%)
  local copies, waits for them, and re-layouts  2.59 us (4%)
    ppermute x6, waiting for transfers between devices, shift(): return lax.ppermute(x, axis, [(i, (i + distance) % n) for i in range(n)])  18.9 us
    ppermute x2, waiting for transfers between devices, body(): lax.ppermute(pair, 'seq', [(i, (i + 4) % count) for i in range(0, count,...  9.11 us
    ppermute x6, starting transfers between devices, shift(): return lax.ppermute(x, axis, [(i, (i + distance) % n) for i in range(n)])  8.86 us
    pallas_call x4, Pallas kernels, attend(): pl.pallas_call(functools.partial(attend_kernel, chunk=chunk, block_len=bl...  7.44 us
    pallas_call x4, Pallas kernels, place(): pl.pallas_call(functools.partial(place_kernel, spots=tuple((e[1:] for e i...  4.94 us
    ppermute x12, starting transfers between devices, partner(): return lax.ppermute(x, axis, [(i, i ^ 1) for i in range(n)])  4.84 us
    ppermute x2, starting transfers between devices, body(): lax.ppermute(pair, 'seq', [(i, (i + 4) % count) for i in range(0, count,...  4.55 us
    pallas_call x2, Pallas kernels, prepare(): pl.pallas_call(functools.partial(prepare_kernel, group=group, block_len=b...  3.63 us
  transfers between devices with their start and end apart: 20, of which 10 were waited for; matrix products, arithmetic and copies ran while one was open for 0% of the time, Pallas kernels for 22%

profile of v2, /device:TPU:0, one launch (start us, length us, event | category | flops | bytes accessed | tf_op | source)
XLA Modules:
  0.0 68.5 jit_solution(2182000703668297848)
XLA Ops:
  0.0 1.0 %slice_bitcast_fusion = (bf16[1,256,128]{2,1,0:T(8,128)(2,1)S(1)}, bf16[1,256,128]{2,1,0:T(8,128)(2,1)S(1)}, bf16[1,256,128]{2,1,0:T(8,128)(2,1)S(1)}, bf16[1,256,128]{2,1,0:T(8,128)(2,1)S(1)}) fusion(bf16[256,256]{1,0:T(8,128)(2,1)} %param.6, bf16[256,256]{1,0:T(8,128)(2,1)} %param.5), kind=kLoop, calls=%fused_computation.2 | loop fusion | bytes 524288 | tf_op jit(solution)/shard_map/stack | solution.py:205
  1.0 3.1 %collective-permute-start.5 = (bf16[2,256,128]{2,1,0:T(8,128)(2,1)S(1)}, bf16[2,256,128]{2,1,0:T(8,128)(2,1)S(1)}, u32[]{:S(2)}, u32[]{:S(2)}) collective-permute-start(bf16[2,256,128]{2,1,0:T(8,128)(2,1)S(1)} %pad_maximum_fusion.1.rest_0_), channel_id=1, source_target_pairs={{0,8},{4,12},{8,16},{12,20},{16,24},{20,28},{24,0},{28,4},{1,9},{5... | collective-permute-start | bytes 393224 | tf_op jit(solution)/shard_map/ppermute | solution.py:26
  4.1 1.5 %collective-permute-start.7 = (bf16[2,256,128]{2,1,0:T(8,128)(2,1)S(1)}, bf16[2,256,128]{2,1,0:T(8,128)(2,1)S(1)}, u32[]{:S(2)}, u32[]{:S(2)}) collective-permute-start(bf16[2,256,128]{2,1,0:T(8,128)(2,1)S(1)} %pad_maximum_fusion.1.rest_0_), channel_id=1, source_target_pairs={{0,4},{4,0},{8,12},{12,8},{16,20},{20,16},{24,28},{28,24},{1,5},{5... | collective-permute-start | bytes 393224 | tf_op jit(solution)/shard_map/ppermute | solution.py:31
  5.6 4.0 %collective-permute-done.5.rest_1_ = bf16[2,256,128]{2,1,0:T(8,128)(2,1)S(1)} collective-permute-done((bf16[2,256,128]{2,1,0:T(8,128)(2,1)S(1)}, bf16[2,256,128]{2,1,0:T(8,128)(2,1)S(1)}, u32[]{:S(2)}, u32[]{:S(2)}) %collective-permute-start.5) | collective-permute-done | bytes 131104 | tf_op jit(solution)/shard_map/ppermute | solution.py:26
  9.6 1.5 %collective-permute-start.6 = (bf16[2,256,128]{2,1,0:T(8,128)(2,1)S(1)}, bf16[2,256,128]{2,1,0:T(8,128)(2,1)S(1)}, u32[]{:S(2)}, u32[]{:S(2)}) collective-permute-start(bf16[2,256,128]{2,1,0:T(8,128)(2,1)S(1)} %collective-permute-done.5.rest_1_), channel_id=1, source_target_pairs={{0,4},{4,0},{8,12},{12,8},{16,20},{20,16},{24,28},{28,24},{1,5},{5... | collective-permute-start | bytes 393224 | tf_op jit(solution)/shard_map/ppermute | solution.py:31
  11.1 0.0 collective-permute-done.7.rest_3_
  11.1 2.6 %collective-permute-start.8 = (bf16[2,256,128]{2,1,0:T(8,128)(2,1)S(1)}, bf16[2,256,128]{2,1,0:T(8,128)(2,1)S(1)}, u32[]{:S(2)}, u32[]{:S(2)}) collective-permute-start(bf16[2,256,128]{2,1,0:T(8,128)(2,1)S(1)} %collective-permute-done.7.rest_3_), channel_id=1, source_target_pairs={{0,16},{8,24},{16,0},{24,8},{1,17},{9,25},{17,1},{25,9},{2,18},{10... | collective-permute-start | bytes 393224 | tf_op jit(solution)/shard_map/ppermute | solution.py:209
  13.8 1.6 %collective-permute-start = (bf16[2,256,128]{2,1,0:T(8,128)(2,1)S(1)}, bf16[2,256,128]{2,1,0:T(8,128)(2,1)S(1)}, u32[]{:S(2)}, u32[]{:S(2)}) collective-permute-start(bf16[2,256,128]{2,1,0:T(8,128)(2,1)S(1)} %pad_maximum_fusion.rest_0_), channel_id=1, source_target_pairs={{0,8},{4,12},{8,16},{12,20},{16,24},{20,28},{24,0},{28,4},{1,9},{5... | collective-permute-start | bytes 393224 | tf_op jit(solution)/shard_map/ppermute | solution.py:26
  15.4 0.0 collective-permute-start.2
  15.4 1.8 %shard_map.47 = (bf16[1024,128]{1,0:T(8,128)(2,1)S(1)}, bf16[1024,128]{1,0:T(8,128)(2,1)S(1)}, bf16[256,1024]{1,0:T(8,128)(2,1)S(1)}) custom-call(s32[16]{0:T(128)} %pos_ref.3, bf16[256,2048]{1,0:T(8,128)(2,1)} %q_ref.3), custom_call_target="tpu_custom_call" | custom-call | tf_op jit(solution)/shard_map/pallas_call | solution.py:78
  17.2 0.0 collective-permute-done.6.rest_2_
  17.2 5.5 %collective-permute-done.8.rest_4_ = bf16[2,256,128]{2,1,0:T(8,128)(2,1)S(1)} collective-permute-done((bf16[2,256,128]{2,1,0:T(8,128)(2,1)S(1)}, bf16[2,256,128]{2,1,0:T(8,128)(2,1)S(1)}, u32[]{:S(2)}, u32[]{:S(2)}) %collective-permute-start.8) | collective-permute-done | bytes 131104 | tf_op jit(solution)/shard_map/ppermute | solution.py:209
  22.8 1.9 %shard_map.51.refs_0_ = bf16[128,1024]{1,0:T(8,128)(2,1)S(1)} custom-call(bf16[1024,128]{1,0:T(8,128)(2,1)S(1)} %get-tuple-element.20.stack_ref, bf16[256,1024]{1,0:T(8,128)(2,1)S(1)} %get-tuple-element.17.mask_ref, bf16[2,256,128]{2,1,0:T(8,128)(2,1)S(1)} %pad_maximum_fusion.1.rest_0_, bf16[2,256,128]{2,1,0:T(8,128)(2,1)S(1)} %collective-permute-done.5.rest_1_, ...), custom_call_target="tpu_custom_call" | custom-call | tf_op jit(solution)/shard_map/pallas_call | solution.py:147
  24.6 1.6 %collective-permute-start.12 = (bf16[128,1024]{1,0:T(8,128)(2,1)S(1)}, bf16[128,1024]{1,0:T(8,128)(2,1)S(1)}, u32[]{:S(2)}, u32[]{:S(2)}) collective-permute-start(bf16[128,1024]{1,0:T(8,128)(2,1)S(1)} %shard_map.51.refs_0_), channel_id=1, source_target_pairs={{0,2},{1,3},{2,0},{3,1},{4,6},{5,7},{6,4},{7,5},{8,10},{9,11},{10,... | collective-permute-start | bytes 786440 | tf_op jit(solution)/shard_map/ppermute | solution.py:26
  26.2 0.0 collective-permute-start.14
  26.2 1.9 %shard_map.49.refs_2_ = bf16[128,1024]{1,0:T(8,128)(2,1)S(1)} custom-call(bf16[1024,128]{1,0:T(8,128)(2,1)S(1)} %get-tuple-element.18.stack_ref, bf16[256,1024]{1,0:T(8,128)(2,1)S(1)} %get-tuple-element.17.mask_ref, bf16[2,256,128]{2,1,0:T(8,128)(2,1)S(1)} %pad_maximum_fusion.1.rest_0_, bf16[2,256,128]{2,1,0:T(8,128)(2,1)S(1)} %collective-permute-done.5.rest_1_, ...), custom_call_target="tpu_custom_call" | custom-call | tf_op jit(solution)/shard_map/pallas_call | solution.py:147
  28.1 0.6 collective-permute-start.15
  28.6 0.0 collective-permute-done.rest_1_
  28.7 0.0 collective-permute-start.1
  28.7 0.0 collective-permute-done.2.rest_3_
  28.7 1.9 %collective-permute-start.3 = (bf16[2,256,128]{2,1,0:T(8,128)(2,1)S(1)}, bf16[2,256,128]{2,1,0:T(8,128)(2,1)S(1)}, u32[]{:S(2)}, u32[]{:S(2)}) collective-permute-start(bf16[2,256,128]{2,1,0:T(8,128)(2,1)S(1)} %collective-permute-done.2.rest_3_), channel_id=1, source_target_pairs={{0,16},{8,24},{16,0},{24,8},{1,17},{9,25},{17,1},{25,9},{2,18},{10... | collective-permute-start | bytes 393224 | tf_op jit(solution)/shard_map/ppermute | solution.py:209
  30.6 1.8 %shard_map.46 = (bf16[1024,128]{1,0:T(8,128)(2,1)S(1)}, bf16[1024,128]{1,0:T(8,128)(2,1)S(1)}) custom-call(s32[16]{0:T(128)} %pos_ref.3, bf16[256,2048]{1,0:T(8,128)(2,1)} %q_ref.3), custom_call_target="tpu_custom_call" | custom-call | tf_op jit(solution)/shard_map/pallas_call | solution.py:78
  32.4 0.0 copy-start
  32.4 0.7 %copy-done = bf16[1024,128]{1,0:T(8,128)(2,1)} copy-done((bf16[1024,128]{1,0:T(8,128)(2,1)}, bf16[1024,128]{1,0:T(8,128)(2,1)S(1)}, u32[]{:S(2)}) %copy-start) | copy-done | bytes 262168
  33.1 1.0 %collective-permute-done.1.rest_2_ = bf16[2,256,128]{2,1,0:T(8,128)(2,1)S(1)} collective-permute-done((bf16[2,256,128]{2,1,0:T(8,128)(2,1)S(1)}, bf16[2,256,128]{2,1,0:T(8,128)(2,1)S(1)}, u32[]{:S(2)}, u32[]{:S(2)}) %collective-permute-start.1) | collective-permute-done | bytes 131104 | tf_op jit(solution)/shard_map/ppermute | solution.py:31
  34.1 3.6 %collective-permute-done.3.rest_4_ = bf16[2,256,128]{2,1,0:T(8,128)(2,1)S(1)} collective-permute-done((bf16[2,256,128]{2,1,0:T(8,128)(2,1)S(1)}, bf16[2,256,128]{2,1,0:T(8,128)(2,1)S(1)}, u32[]{:S(2)}, u32[]{:S(2)}) %collective-permute-start.3) | collective-permute-done | bytes 131104 | tf_op jit(solution)/shard_map/ppermute | solution.py:209
  37.7 1.9 %shard_map.50.refs_0_ = bf16[128,1024]{1,0:T(8,128)(2,1)S(1)} custom-call(bf16[1024,128]{1,0:T(8,128)(2,1)S(1)} %get-tuple-element.19.stack_ref, bf16[256,1024]{1,0:T(8,128)(2,1)S(1)} %get-tuple-element.17.mask_ref, bf16[2,256,128]{2,1,0:T(8,128)(2,1)S(1)} %pad_maximum_fusion.rest_0_, bf16[2,256,128]{2,1,0:T(8,128)(2,1)S(1)} %collective-permute-done.rest_1_, ...), custom_call_target="tpu_custom_call" | custom-call | tf_op jit(solution)/shard_map/pallas_call | solution.py:147
  39.6 0.1 collective-permute-start.10
  39.7 0.0 copy-start.1
  39.7 0.9 %copy-done.1 = bf16[1024,128]{1,0:T(8,128)(2,1)S(1)} copy-done((bf16[1024,128]{1,0:T(8,128)(2,1)S(1)}, bf16[1024,128]{1,0:T(8,128)(2,1)}, u32[]{:S(2)}) %copy-start.1) | copy-done | bytes 262168
  40.6 1.9 %shard_map.48.refs_2_ = bf16[128,1024]{1,0:T(8,128)(2,1)S(1)} custom-call(bf16[1024,128]{1,0:T(8,128)(2,1)S(1)} %copy-done.1, bf16[256,1024]{1,0:T(8,128)(2,1)S(1)} %get-tuple-element.17.mask_ref, bf16[2,256,128]{2,1,0:T(8,128)(2,1)S(1)} %pad_maximum_fusion.rest_0_, bf16[2,256,128]{2,1,0:T(8,128)(2,1)S(1)} %collective-permute-done.rest_1_, ...), custom_call_target="tpu_custom_call" | custom-call | tf_op jit(solution)/shard_map/pallas_call | solution.py:147
  42.5 0.6 collective-permute-start.11
  43.0 0.0 collective-permute-done.12.refs_4_
  43.0 0.1 collective-permute-start.13
  43.1 0.0 collective-permute-done.14.refs_1_
  43.1 0.5 collective-permute-start.9
  43.7 0.0 collective-permute-done.15.refs_3_
  43.7 1.5 %collective-permute-start.17 = (bf16[128,1024]{1,0:T(8,128)(2,1)S(1)}, bf16[128,1024]{1,0:T(8,128)(2,1)S(1)}, u32[]{:S(2)}, u32[]{:S(2)}) collective-permute-start(bf16[128,1024]{1,0:T(8,128)(2,1)S(1)} %shard_map.50.refs_0_), channel_id=1, source_target_pairs={{0,2},{1,3},{2,0},{3,1},{4,6},{5,7},{6,4},{7,5},{8,10},{9,11},{10,... | collective-permute-start | bytes 786440 | tf_op jit(solution)/shard_map/ppermute | solution.py:26
  45.2 1.9 %place.4.refs_6_ = bf16[256,8192]{1,0:T(8,128)(2,1)} custom-call(bf16[128,1024]{1,0:T(8,128)(2,1)S(1)} %shard_map.51.refs_0_, bf16[128,1024]{1,0:T(8,128)(2,1)} %collective-permute-done.14.refs_1_, bf16[128,1024]{1,0:T(8,128)(2,1)S(1)} %shard_map.49.refs_2_, bf16[128,1024]{1,0:T(8,128)(2,1)S(1)} %collective-permute-done.15.refs_3_), custom_call_target="tpu_custom_call" | custom-call | tf_op jit(solution)/shard_map/place/pallas_call | solution.py:182
  47.1 0.0 collective-permute-done.10.refs_1_
  47.1 0.0 collective-permute-done.11.refs_3_
  47.1 0.0 collective-permute-done.13.refs_5_
  47.1 1.2 %place.5.refs_4_ = bf16[256,8192]{1,0:T(8,128)(2,1)} custom-call(bf16[128,1024]{1,0:T(8,128)(2,1)S(1)} %shard_map.50.refs_0_, bf16[128,1024]{1,0:T(8,128)(2,1)S(1)} %collective-permute-done.10.refs_1_, bf16[128,1024]{1,0:T(8,128)(2,1)S(1)} %shard_map.48.refs_2_, ...), custom_call_target="tpu_custom_call", output_to_operand_aliasing={{}: (6, {})} | custom-call | tf_op jit(solution)/shard_map/place/pallas_call | solution.py:182
  48.4 4.0 %collective-permute-done.9.refs_0_ = bf16[128,1024]{1,0:T(8,128)(2,1)S(1)} collective-permute-done((bf16[128,1024]{1,0:T(8,128)(2,1)S(1)}, bf16[128,1024]{1,0:T(8,128)(2,1)S(1)}, u32[]{:S(2)}, u32[]{:S(2)}) %collective-permute-start.9) | collective-permute-done | bytes 262176 | tf_op jit(solution)/shard_map/ppermute | solution.py:26
  52.3 5.1 %collective-permute-done.17.refs_2_ = bf16[128,1024]{1,0:T(8,128)(2,1)S(1)} collective-permute-done((bf16[128,1024]{1,0:T(8,128)(2,1)S(1)}, bf16[128,1024]{1,0:T(8,128)(2,1)S(1)}, u32[]{:S(2)}, u32[]{:S(2)}) %collective-permute-start.17) | collective-permute-done | bytes 262176 | tf_op jit(solution)/shard_map/ppermute | solution.py:26
  57.4 0.0 collective-permute-start.18
  57.4 0.5 collective-permute-start.16
  57.9 0.5 collective-permute-start.4
  58.4 0.5 collective-permute-done.18.refs_3_
  58.9 0.4 collective-permute-done.16.refs_1_
  59.3 1.0 %place.6.refs_2_ = bf16[256,8192]{1,0:T(8,128)(2,1)} custom-call(bf16[128,1024]{1,0:T(8,128)(2,1)S(1)} %collective-permute-done.9.refs_0_, bf16[128,1024]{1,0:T(8,128)(2,1)S(1)} %collective-permute-done.16.refs_1_, bf16[128,1024]{1,0:T(8,128)(2,1)S(1)} %collective-permute-done.17.refs_2_, ...), custom_call_target="tpu_custom_call", output_to_operand_aliasing={{}: (4, {})} | custom-call | tf_op jit(solution)/shard_map/place/pallas_call | solution.py:182
  60.3 5.8 %collective-permute-done.4.refs_0_ = bf16[128,1024]{1,0:T(8,128)(2,1)S(1)} collective-permute-done((bf16[128,1024]{1,0:T(8,128)(2,1)S(1)}, bf16[128,1024]{1,0:T(8,128)(2,1)S(1)}, u32[]{:S(2)}, u32[]{:S(2)}) %collective-permute-start.4) | collective-permute-done | bytes 262176 | tf_op jit(solution)/shard_map/ppermute | solution.py:26
  66.1 0.0 collective-permute-start.19
  66.1 1.5 %collective-permute-done.19.refs_1_ = bf16[128,1024]{1,0:T(8,128)(2,1)S(1)} collective-permute-done((bf16[128,1024]{1,0:T(8,128)(2,1)S(1)}, bf16[128,1024]{1,0:T(8,128)(2,1)S(1)}, u32[]{:S(2)}, u32[]{:S(2)}) %collective-permute-start.19) | collective-permute-done | bytes 262176 | tf_op jit(solution)/shard_map/ppermute | solution.py:31
  67.7 0.8 %place.7 = bf16[256,8192]{1,0:T(8,128)(2,1)} custom-call(bf16[128,1024]{1,0:T(8,128)(2,1)S(1)} %collective-permute-done.4.refs_0_, bf16[128,1024]{1,0:T(8,128)(2,1)S(1)} %collective-permute-done.19.refs_1_, bf16[256,8192]{1,0:T(8,128)(2,1)} %place.6.refs_2_), custom_call_target="tpu_custom_call", output_to_operand_aliasing={{}: (2, {})} | custom-call | tf_op jit(solution)/shard_map/place/pallas_call | solution.py:182
  (2 shorter events, 0.0 us)
Async XLA Ops:
  1.0 8.6 %collective-permute-start.5 = (bf16[2,256,128]{2,1,0:T(8,128)(2,1)S(1)}, bf16[2,256,128]{2,1,0:T(8,128)(2,1)S(1)}, u32[]{:S(2)}, u32[]{:S(2)}) collective-permute-start(bf16[2,256,128]{2,1,0:T(8,128)(2,1)S(1)} %pad_maximum_fusion.1.rest_0_), channel_id=1, source_target_pairs={{0,8},{4,12},{8,16},{12,20},{16,24},{20,28},{24,0},{28,4},{1,9},{5... | collective-permute-start | bytes 393224 | tf_op jit(solution)/shard_map/ppermute | solution.py:26
  4.1 7.0 %collective-permute-start.7 = (bf16[2,256,128]{2,1,0:T(8,128)(2,1)S(1)}, bf16[2,256,128]{2,1,0:T(8,128)(2,1)S(1)}, u32[]{:S(2)}, u32[]{:S(2)}) collective-permute-start(bf16[2,256,128]{2,1,0:T(8,128)(2,1)S(1)} %pad_maximum_fusion.1.rest_0_), channel_id=1, source_target_pairs={{0,4},{4,0},{8,12},{12,8},{16,20},{20,16},{24,28},{28,24},{1,5},{5... | collective-permute-start | bytes 393224 | tf_op jit(solution)/shard_map/ppermute | solution.py:31
  9.6 7.6 %collective-permute-start.6 = (bf16[2,256,128]{2,1,0:T(8,128)(2,1)S(1)}, bf16[2,256,128]{2,1,0:T(8,128)(2,1)S(1)}, u32[]{:S(2)}, u32[]{:S(2)}) collective-permute-start(bf16[2,256,128]{2,1,0:T(8,128)(2,1)S(1)} %collective-permute-done.5.rest_1_), channel_id=1, source_target_pairs={{0,4},{4,0},{8,12},{12,8},{16,20},{20,16},{24,28},{28,24},{1,5},{5... | collective-permute-start | bytes 393224 | tf_op jit(solution)/shard_map/ppermute | solution.py:31
  11.1 11.7 %collective-permute-start.8 = (bf16[2,256,128]{2,1,0:T(8,128)(2,1)S(1)}, bf16[2,256,128]{2,1,0:T(8,128)(2,1)S(1)}, u32[]{:S(2)}, u32[]{:S(2)}) collective-permute-start(bf16[2,256,128]{2,1,0:T(8,128)(2,1)S(1)} %collective-permute-done.7.rest_3_), channel_id=1, source_target_pairs={{0,16},{8,24},{16,0},{24,8},{1,17},{9,25},{17,1},{25,9},{2,18},{10... | collective-permute-start | bytes 393224 | tf_op jit(solution)/shard_map/ppermute | solution.py:209
  13.8 14.9 %collective-permute-start = (bf16[2,256,128]{2,1,0:T(8,128)(2,1)S(1)}, bf16[2,256,128]{2,1,0:T(8,128)(2,1)S(1)}, u32[]{:S(2)}, u32[]{:S(2)}) collective-permute-start(bf16[2,256,128]{2,1,0:T(8,128)(2,1)S(1)} %pad_maximum_fusion.rest_0_), channel_id=1, source_target_pairs={{0,8},{4,12},{8,16},{12,20},{16,24},{20,28},{24,0},{28,4},{1,9},{5... | collective-permute-start | bytes 393224 | tf_op jit(solution)/shard_map/ppermute | solution.py:26
  15.4 13.2 %collective-permute-start.2 = (bf16[2,256,128]{2,1,0:T(8,128)(2,1)S(1)}, bf16[2,256,128]{2,1,0:T(8,128)(2,1)S(1)}, u32[]{:S(2)}, u32[]{:S(2)}) collective-permute-start(bf16[2,256,128]{2,1,0:T(8,128)(2,1)S(1)} %pad_maximum_fusion.rest_0_), channel_id=1, source_target_pairs={{0,4},{4,0},{8,12},{12,8},{16,20},{20,16},{24,28},{28,24},{1,5},{5... | collective-permute-start | bytes 393224 | tf_op jit(solution)/shard_map/ppermute | solution.py:31
  24.6 18.4 %collective-permute-start.12 = (bf16[128,1024]{1,0:T(8,128)(2,1)S(1)}, bf16[128,1024]{1,0:T(8,128)(2,1)S(1)}, u32[]{:S(2)}, u32[]{:S(2)}) collective-permute-start(bf16[128,1024]{1,0:T(8,128)(2,1)S(1)} %shard_map.51.refs_0_), channel_id=1, source_target_pairs={{0,2},{1,3},{2,0},{3,1},{4,6},{5,7},{6,4},{7,5},{8,10},{9,11},{10,... | collective-permute-start | bytes 786440 | tf_op jit(solution)/shard_map/ppermute | solution.py:26
  26.2 16.9 %collective-permute-start.14 = (bf16[128,1024]{1,0:T(8,128)(2,1)S(1)}, bf16[128,1024]{1,0:T(8,128)(2,1)}, u32[]{:S(2)}, u32[]{:S(2)}) collective-permute-start(bf16[128,1024]{1,0:T(8,128)(2,1)S(1)} %shard_map.51.refs_0_), channel_id=1, source_target_pairs={{0,1},{1,0},{2,3},{3,2},{4,5},{5,4},{6,7},{7,6},{8,9},{9,8},{10,11... | collective-permute-start | bytes 786440 | tf_op jit(solution)/shard_map/ppermute | solution.py:31
  28.1 15.6 %collective-permute-start.15 = (bf16[128,1024]{1,0:T(8,128)(2,1)S(1)}, bf16[128,1024]{1,0:T(8,128)(2,1)S(1)}, u32[]{:S(2)}, u32[]{:S(2)}) collective-permute-start(bf16[128,1024]{1,0:T(8,128)(2,1)S(1)} %shard_map.49.refs_2_), channel_id=1, source_target_pairs={{0,1},{1,0},{2,3},{3,2},{4,5},{5,4},{6,7},{7,6},{8,9},{9,8},{10,11... | collective-permute-start | bytes 786440 | tf_op jit(solution)/shard_map/ppermute | solution.py:31
  28.7 5.5 %collective-permute-start.1 = (bf16[2,256,128]{2,1,0:T(8,128)(2,1)S(1)}, bf16[2,256,128]{2,1,0:T(8,128)(2,1)S(1)}, u32[]{:S(2)}, u32[]{:S(2)}) collective-permute-start(bf16[2,256,128]{2,1,0:T(8,128)(2,1)S(1)} %collective-permute-done.rest_1_), channel_id=1, source_target_pairs={{0,4},{4,0},{8,12},{12,8},{16,20},{20,16},{24,28},{28,24},{1,5},{5... | collective-permute-start | bytes 393224 | tf_op jit(solution)/shard_map/ppermute | solution.py:31
  28.7 9.1 %collective-permute-start.3 = (bf16[2,256,128]{2,1,0:T(8,128)(2,1)S(1)}, bf16[2,256,128]{2,1,0:T(8,128)(2,1)S(1)}, u32[]{:S(2)}, u32[]{:S(2)}) collective-permute-start(bf16[2,256,128]{2,1,0:T(8,128)(2,1)S(1)} %collective-permute-done.2.rest_3_), channel_id=1, source_target_pairs={{0,16},{8,24},{16,0},{24,8},{1,17},{9,25},{17,1},{25,9},{2,18},{10... | collective-permute-start | bytes 393224 | tf_op jit(solution)/shard_map/ppermute | solution.py:209
  32.4 0.7 %copy-start = (bf16[1024,128]{1,0:T(8,128)(2,1)}, bf16[1024,128]{1,0:T(8,128)(2,1)S(1)}, u32[]{:S(2)}) copy-start(bf16[1024,128]{1,0:T(8,128)(2,1)S(1)} %get-tuple-element.16.stack_ref) | copy-start | bytes 786436
  39.6 7.5 %collective-permute-start.10 = (bf16[128,1024]{1,0:T(8,128)(2,1)S(1)}, bf16[128,1024]{1,0:T(8,128)(2,1)S(1)}, u32[]{:S(2)}, u32[]{:S(2)}) collective-permute-start(bf16[128,1024]{1,0:T(8,128)(2,1)S(1)} %shard_map.50.refs_0_), channel_id=1, source_target_pairs={{0,1},{1,0},{2,3},{3,2},{4,5},{5,4},{6,7},{7,6},{8,9},{9,8},{10,11... | collective-permute-start | bytes 786440 | tf_op jit(solution)/shard_map/ppermute | solution.py:31
  39.7 1.0 %copy-start.1 = (bf16[1024,128]{1,0:T(8,128)(2,1)S(1)}, bf16[1024,128]{1,0:T(8,128)(2,1)}, u32[]{:S(2)}) copy-start(bf16[1024,128]{1,0:T(8,128)(2,1)} %copy-done) | copy-start | bytes 786436
  42.5 4.6 %collective-permute-start.11 = (bf16[128,1024]{1,0:T(8,128)(2,1)S(1)}, bf16[128,1024]{1,0:T(8,128)(2,1)S(1)}, u32[]{:S(2)}, u32[]{:S(2)}) collective-permute-start(bf16[128,1024]{1,0:T(8,128)(2,1)S(1)} %shard_map.48.refs_2_), channel_id=1, source_target_pairs={{0,1},{1,0},{2,3},{3,2},{4,5},{5,4},{6,7},{7,6},{8,9},{9,8},{10,11... | collective-permute-start | bytes 786440 | tf_op jit(solution)/shard_map/ppermute | solution.py:31
  43.0 4.1 %collective-permute-start.13 = (bf16[128,1024]{1,0:T(8,128)(2,1)S(1)}, bf16[128,1024]{1,0:T(8,128)(2,1)S(1)}, u32[]{:S(2)}, u32[]{:S(2)}) collective-permute-start(bf16[128,1024]{1,0:T(8,128)(2,1)S(1)} %collective-permute-done.12.refs_4_), channel_id=1, source_target_pairs={{0,1},{1,0},{2,3},{3,2},{4,5},{5,4},{6,7},{7,6},{8,9},{9,8},{10,11... | collective-permute-start | bytes 786440 | tf_op jit(solution)/shard_map/ppermute | solution.py:31
  43.1 9.2 %collective-permute-start.9 = (bf16[128,1024]{1,0:T(8,128)(2,1)S(1)}, bf16[128,1024]{1,0:T(8,128)(2,1)S(1)}, u32[]{:S(2)}, u32[]{:S(2)}) collective-permute-start(bf16[128,1024]{1,0:T(8,128)(2,1)S(1)} %shard_map.49.refs_2_), channel_id=1, source_target_pairs={{0,2},{1,3},{2,0},{3,1},{4,6},{5,7},{6,4},{7,5},{8,10},{9,11},{10,... | collective-permute-start | bytes 786440 | tf_op jit(solution)/shard_map/ppermute | solution.py:26
  43.7 13.7 %collective-permute-start.17 = (bf16[128,1024]{1,0:T(8,128)(2,1)S(1)}, bf16[128,1024]{1,0:T(8,128)(2,1)S(1)}, u32[]{:S(2)}, u32[]{:S(2)}) collective-permute-start(bf16[128,1024]{1,0:T(8,128)(2,1)S(1)} %shard_map.50.refs_0_), channel_id=1, source_target_pairs={{0,2},{1,3},{2,0},{3,1},{4,6},{5,7},{6,4},{7,5},{8,10},{9,11},{10,... | collective-permute-start | bytes 786440 | tf_op jit(solution)/shard_map/ppermute | solution.py:26
  57.4 1.5 %collective-permute-start.18 = (bf16[128,1024]{1,0:T(8,128)(2,1)S(1)}, bf16[128,1024]{1,0:T(8,128)(2,1)S(1)}, u32[]{:S(2)}, u32[]{:S(2)}) collective-permute-start(bf16[128,1024]{1,0:T(8,128)(2,1)S(1)} %collective-permute-done.17.refs_2_), channel_id=1, source_target_pairs={{0,1},{1,0},{2,3},{3,2},{4,5},{5,4},{6,7},{7,6},{8,9},{9,8},{10,11... | collective-permute-start | bytes 786440 | tf_op jit(solution)/shard_map/ppermute | solution.py:31
  57.4 1.9 %collective-permute-start.16 = (bf16[128,1024]{1,0:T(8,128)(2,1)S(1)}, bf16[128,1024]{1,0:T(8,128)(2,1)S(1)}, u32[]{:S(2)}, u32[]{:S(2)}) collective-permute-start(bf16[128,1024]{1,0:T(8,128)(2,1)S(1)} %collective-permute-done.9.refs_0_), channel_id=1, source_target_pairs={{0,1},{1,0},{2,3},{3,2},{4,5},{5,4},{6,7},{7,6},{8,9},{9,8},{10,11... | collective-permute-start | bytes 786440 | tf_op jit(solution)/shard_map/ppermute | solution.py:31
  57.9 8.2 %collective-permute-start.4 = (bf16[128,1024]{1,0:T(8,128)(2,1)S(1)}, bf16[128,1024]{1,0:T(8,128)(2,1)S(1)}, u32[]{:S(2)}, u32[]{:S(2)}) collective-permute-start(bf16[128,1024]{1,0:T(8,128)(2,1)S(1)} %shard_map.48.refs_2_), channel_id=1, source_target_pairs={{0,2},{1,3},{2,0},{3,1},{4,6},{5,7},{6,4},{7,5},{8,10},{9,11},{10,... | collective-permute-start | bytes 786440 | tf_op jit(solution)/shard_map/ppermute | solution.py:26
  66.1 1.5 %collective-permute-start.19 = (bf16[128,1024]{1,0:T(8,128)(2,1)S(1)}, bf16[128,1024]{1,0:T(8,128)(2,1)S(1)}, u32[]{:S(2)}, u32[]{:S(2)}) collective-permute-start(bf16[128,1024]{1,0:T(8,128)(2,1)S(1)} %collective-permute-done.4.refs_0_), channel_id=1, source_target_pairs={{0,1},{1,0},{2,3},{3,2},{4,5},{5,4},{6,7},{7,6},{8,9},{9,8},{10,11... | collective-permute-start | bytes 786440 | tf_op jit(solution)/shard_map/ppermute | solution.py:31
